TPU v7x, 128 devices: a whole 4x4x4 slice. The times are simulated.
128 devices in a mesh: dp: 4 (over x), vocab: 32 (over z, y, core).
Axes of the slice: x: 4, y: 4, z: 4, core: 2. Of those that a mesh axis runs over, the one named last changes fastest.
Arguments:
- token_ids: int32 [524288], P(('dp', 'vocab')), may hold values from 0 to 30719, as said below
- valid_counts: int32 [4096], P(('dp', 'vocab')), may hold values from 64 to 128
- grad_output: bfloat16 [524288, 768], P(('dp', 'vocab')), may hold values from -6 to 6
- pre_norm: bfloat16 [524288, 768], P(('dp', 'vocab')), may hold values from -6 to 6
- norm_gain: float32 [768], replicated, may hold values from 0.5 to 1.5
Outputs:
- grad_table: float32 [30720, 768], P('vocab')
Inputs may be any that keep to these rules, and one draw needn't show every extreme that they name: `token_ids`: of the 4096 positions of one device, at most 256 have ids in any one range [k * 960, (k + 1) * 960); in every group of 32 consecutive devices one such range takes exactly 256 from every device of the group. Padding positions carry ids too.
All inputs are finite; a program needn't handle non-finite values.
Results may differ from a plain program's by a relative error of at most 0.0029.
Values may be sent and summed in bfloat16 or wider, within the bound.
A program may use at most 128 MiB of HBM per device.

v0:
```python
import jax
import jax.numpy as jnp
from jax import lax
from jax.sharding import PartitionSpec as P

VOCAB_DEV = 960
BLOCK = 128


def row_grads(grads, values, counts, gain):
    x = values.astype(jnp.float32)
    mu = jnp.mean(x, axis=1, keepdims=True)
    centered_input = x - mu
    inverse_deviation = lax.rsqrt(
        jnp.mean(centered_input * centered_input, axis=1, keepdims=True) + 1e-12
    )
    normalized_input = centered_input * inverse_deviation
    scaled_gradient = gain[None, :] * grads.astype(jnp.float32)
    first_term = jnp.mean(scaled_gradient, axis=1, keepdims=True)
    second_term = jnp.mean(scaled_gradient * normalized_input, axis=1, keepdims=True)
    input_gradient = inverse_deviation * (
        scaled_gradient - first_term - normalized_input * second_term
    )
    place = jnp.arange(x.shape[0], dtype=jnp.int32) % BLOCK
    alive = place < jnp.repeat(counts, BLOCK)
    return (jnp.where(alive[:, None], input_gradient, 0.0).astype(jnp.bfloat16), alive)


def per_device(token_ids, valid_counts, grad_output, pre_norm, norm_gain):
    tok_count = token_ids.shape[0]
    width = grad_output.shape[1]
    shards = lax.axis_size("vocab")
    per_owner = 2 * tok_count // shards
    rows, alive = row_grads(grad_output, pre_norm, valid_counts, norm_gain)
    owner = token_ids // VOCAB_DEV
    within = token_ids % VOCAB_DEV
    marks = (owner[:, None] == jnp.arange(shards, dtype=jnp.int32)[None, :]).astype(jnp.int32)
    rank = jnp.sum((jnp.cumsum(marks, axis=0) - 1) * marks, axis=1)
    target = owner * per_owner + rank
    outbox = jnp.zeros((shards * per_owner, width), jnp.bfloat16).at[target].set(rows)
    labels = (
        jnp.full((shards * per_owner,), -1, jnp.int32).at[target].set(jnp.where(alive, within, -1))
    )
    outbox = outbox.reshape(shards, per_owner, width)
    labels = labels.reshape(shards, per_owner)
    inbox, inlabels = (
        lax.all_to_all(outbox, "vocab", split_axis=0, concat_axis=0, tiled=True),
        lax.all_to_all(labels, "vocab", split_axis=0, concat_axis=0, tiled=True),
    )
    inbox = inbox.reshape(shards * per_owner, width)
    inlabels = inlabels.reshape(shards * per_owner)
    picker = (jnp.arange(VOCAB_DEV, dtype=jnp.int32)[:, None] == inlabels[None, :]).astype(
        jnp.bfloat16
    )
    partial_table = jnp.dot(picker, inbox, preferred_element_type=jnp.float32)
    table = lax.psum(partial_table, "dp")
    return table


def solution(mesh):
    in_specs = (
        P(("dp", "vocab")),
        P(("dp", "vocab")),
        P(("dp", "vocab"), None),
        P(("dp", "vocab"), None),
        P(),
    )
    out_specs = P("vocab", None)
    return jax.shard_map(
        per_device, mesh=mesh, in_specs=in_specs, out_specs=out_specs, check_vma=False
    )
```

profile of v0, /device:TPU:2, one launch (start us, length us, event | category | flops | bytes accessed | tf_op | source)
XLA Modules:
  0.0 329.1 jit_solution(7814792259290701923)
XLA Ops:
  6.5 0.7 add_select_fusion.2
  7.3 0.1 fusion.25
  7.3 9.2 %reduce-window.6 = s32[32,32,128]{2,1,0:T(8,128)S(1)} reduce-window(s32[32,32,128]{2,1,0:T(8,128)S(1)} %fusion.25, s32[]{:T(128)} %constant.52.clone.1), window={size=1x1x128 pad=0_0x0_0x127_0}, to_apply=%region_0.0 | reduce-window | flops 16646144 | bytes 1048580 | tf_op jit(solution)/shard_map/reduce-window
  16.6 0.8 slice_reduce_fusion
  17.4 0.2 reduce-window.9
  17.6 0.2 add_add_fusion
  17.8 0.3 fusion.24
  18.1 0.8 fusion.27
  18.9 16.1 %scatter_custom_fusion = s32[8192]{0:T(1024)} fusion(s32[4096]{0:T(1024)S(1)} %get-tuple-element.8, s32[4096]{0:T(1024)S(1)} %get-tuple-element.7, s32[]{:T(128)} %constant.49.clone.1), kind=kCustom, calls=%fused_computation.47 | custom fusion | bytes 32772 | tf_op jit(solution)/shard_map/scatter | solution.py:42
  35.0 8.3 %all-to-all-start = ((s32[32,1,256]{2,1,0:T(1,128)}), s32[32,1,256]{2,1,0:T(1,128)S(1)}, u32[]{:S(2)}, u32[]{:S(2)}) async-start(s32[32,1,256]{2,1,0:T(1,128)} %bitcast.3), calls=%async_computation | async-start | bytes 65536 | tf_op jit(solution)/shard_map/all_to_all | solution.py:48
  43.3 0.0 copy-start.3
  43.3 0.2 all-reduce.2.cloned.1.call-start
  43.6 0.0 copy-start
  43.6 0.0 copy-start.1
  43.6 3.8 %convert_reduce_fusion = f32[4096]{0:T(1024)S(1)} fusion(bf16[4096,768]{1,0:T(8,128)(2,1)} %param.8), kind=kLoop, calls=%fused_computation.5 | loop fusion | flops 6287360 | bytes 6307840 | tf_op jit(solution)/shard_map/reduce_sum | solution.py:12
  47.5 5.4 %fusion.11 = f32[4096]{0:T(1024)S(1)} fusion(bf16[4096,768]{1,0:T(8,128)(2,1)} %param.8, f32[4096]{0:T(1024)S(1)} %broadcast_multiply_fusion.2), kind=kLoop, calls=%fused_computation.16 | loop fusion | flops 12578816 | bytes 6324224 | tf_op jit(solution)/shard_map/reduce_sum | solution.py:15
  52.9 4.7 %fusion.12 = (f32[4096]{0:T(1024)S(1)}, f32[4096]{0:T(1024)S(1)}) fusion(bf16[4096,768]{1,0:T(8,128)(2,1)S(1)} %copy-done.1, f32[768]{0:T(1024)S(1)} %copy-done.2, f32[4096]{0:T(1024)S(1)} %add_rsqrt_fusion, f32[4096]{0:T(1024)S(1)} %broadcast_multiply_fusion.2, bf16[4096,768]{1,0:T(8,128)(2,1)S(1)} %copy-done), kind=kLoop, calls=%fused_computation.18 | loop fusion | flops 25157632 | bytes 12651520 | tf_op jit(solution)/shard_map/reduce_sum | solution.py:19
  57.6 0.1 fusion.26
  57.7 28.5 %scatter_custom_fusion.1 = bf16[8192,768]{1,0:T(8,128)(2,1)} fusion(s32[4096]{0:T(1024)S(1)} %get-tuple-element.8, bf16[4096,768]{1,0:T(8,128)(2,1)} %param.8, bf16[4096,768]{1,0:T(8,128)(2,1)} %param.7, f32[]{:T(128)} %constant.58.clone.1, f32[4096]{0:T(1024)S(1)} %get-tuple-element.11, f32[4096]{0:T(1024)S(1)} %get-tuple-element.12, ...), kind=kCustom, calls=%fused_computation.19 | custom fusion | flops 31457280 | bytes 25239558 | tf_op jit(solution)/shard_map/scatter | solution.py:40
  86.2 148.2 %all_to_all.14 = bf16[32,256,768]{2,1,0:T(8,128)(2,1)S(1)} all-to-all(bf16[32,256,768]{2,1,0:T(8,128)(2,1)} %bitcast.27), channel_id=1, replica_groups=mesh['dp'=4,'vocab'=32] {'vocab'}, dimensions={0} | all-to-all | bytes 25165824 | tf_op jit(solution)/shard_map/all_to_all | solution.py:47
  234.3 15.1 %fusion = f32[960,768]{1,0:T(8,128)} fusion(bf16[8192,768]{1,0:T(8,128)(2,1)S(1)} %bitcast.28, s32[8192]{0:T(1024)S(1)} %bitcast.31), kind=kOutput, calls=%fused_computation.3 | convolution fusion | flops 12087459840 | bytes 15564800 | tf_op jit(solution)/shard_map/dot_general | solution.py:55
  249.4 0.0 all-reduce.2.cloned.1.call-update
  249.5 69.2 %all-reduce.2.cloned.1.call-done = f32[960,768]{1,0:T(8,128)} async-done(((f32[960,768]{1,0:T(8,128)}), f32[960,768]{1,0:T(8,128)}) %all-reduce.2.cloned.1.call-update) | async-done | bytes 2949136 | tf_op jit(solution)/shard_map/psum | solution.py:56
  318.7 3.6 %copy.9 = f32[960,768]{1,0:T(8,128)} copy(f32[960,768]{1,0:T(8,128)} %all-reduce.2.cloned.1.call-done) | data formatting | bytes 5898240
  (9 shorter events, 0.0 us)
Async XLA Ops:
  6.5 46.4 %copy-start.2 = (f32[768]{0:T(1024)S(1)}, f32[768]{0:T(1024)}, u32[]{:S(2)}) copy-start(f32[768]{0:T(1024)} %param.9) | copy-start | bytes 9220
  35.0 51.2 %all-to-all-start = ((s32[32,1,256]{2,1,0:T(1,128)}), s32[32,1,256]{2,1,0:T(1,128)S(1)}, u32[]{:S(2)}, u32[]{:S(2)}) async-start(s32[32,1,256]{2,1,0:T(1,128)} %bitcast.3), calls=%async_computation | async-start | bytes 65536 | tf_op jit(solution)/shard_map/all_to_all | solution.py:48
  43.3 14.3 %copy-start.3 = (s32[32]{0:T(128)S(1)}, s32[32]{0:T(128)}, u32[]{:S(2)}) copy-start(s32[32]{0:T(128)} %param.6) | copy-start | bytes 388
  43.3 275.3 %all-reduce.2.cloned.1.call-start = ((), (), s32[]{:S(2)}) async-start(), calls=%async_computation.2 | async-start | bytes 5898240 | tf_op jit(solution)/shard_map/psum | solution.py:56
  43.6 9.3 %copy-start = (bf16[4096,768]{1,0:T(8,128)(2,1)S(1)}, bf16[4096,768]{1,0:T(8,128)(2,1)}, u32[]{:S(2)}) copy-start(bf16[4096,768]{1,0:T(8,128)(2,1)} %param.8) | copy-start | bytes 18874372
  43.6 9.3 %copy-start.1 = (bf16[4096,768]{1,0:T(8,128)(2,1)S(1)}, bf16[4096,768]{1,0:T(8,128)(2,1)}, u32[]{:S(2)}) copy-start(bf16[4096,768]{1,0:T(8,128)(2,1)} %param.7) | copy-start | bytes 18874372
Sparse Core Ops, SparseCore 0:
  249.6 69.0 all-reduce.1
where the time goes:
time: 331 us; the launch traced here: 329 us
  blocking collectives  148 us (45%)
  waiting for transfers between devices  69.2 us (21%)
  other arithmetic  54 us (16%)
  local copies, waits for them, and re-layouts  20.5 us (6%)
  matrix products  15.1 us (5%)
  between operations  13.5 us (4%)
  starting transfers between devices  8.56 us (3%)
    all_to_all x1, blocking collectives, per_device(): lax.all_to_all(outbox, 'vocab', split_axis=0, concat_axis=0, tiled=True)  148 us
    psum x1, waiting for transfers between devices, per_device(): table = lax.psum(partial_table, 'dp')  69.2 us
    scatter x1, other arithmetic, per_device(): jnp.zeros((shards * per_owner, width), jnp.bfloat16).at[target].set(rows)  28.5 us
    scatter x1, local copies, waits for them, and re-layouts, per_device(): jnp.full((shards * per_owner,), -1, jnp.int32).at[target]  16.1 us
    dot_general x1, matrix products, per_device(): partial_table = jnp.dot(picker, inbox, preferred_element_type=jnp.float32)  15.1 us
    another operation x2, other arithmetic  9.41 us
    all_to_all x1, starting transfers between devices, per_device(): lax.all_to_all(labels, 'vocab', split_axis=0, concat_axis=0, tiled=True)  8.33 us
  transfers between devices with their start and end apart: 2, of which 1 were waited for; matrix products, arithmetic and copies ran while one was open for 13% of the time, Pallas kernels for 0%

commit v1 on v0

v1 whole, which is shorter than its diff:
```python
import functools

import jax
import jax.numpy as jnp
from jax import lax
from jax.experimental import pallas as pl
from jax.experimental.pallas import tpu as pltpu
from jax.sharding import PartitionSpec as P

VOCAB_DEV = 960
BLOCK = 128
CAP = 256
QROWS = VOCAB_DEV // 4
MESH = pl.DeviceIdType.MESH
F32, BF16, I32 = jnp.float32, jnp.bfloat16, jnp.int32


def place():
    x = lax.axis_index("dp")
    v = lax.axis_index("vocab")
    return x, v // 8, (v // 2) % 4, v % 2


def device(x, z, y, c):
    return (x, z * 8 + y * 2 + c)


def shifted(axis, d, dc=0):
    x, z, y, c = place()
    c = (c + dc) % 2
    if axis == "x":
        return device((x + d) % 4, z, y, c)
    if axis == "y":
        return device(x, z, (y + d) % 4, c)
    return device(x, (z + d) % 4, y, c)


def coordinate(axis):
    x, z, y, _ = place()
    return {"x": x, "y": y, "z": z}[axis]


def routing(token_ids, valid_counts):
    toks = token_ids.shape[0]
    blocks = toks // BLOCK
    owner = token_ids // VOCAB_DEV
    within = token_ids - owner * VOCAB_DEV
    place_in = jnp.arange(toks, dtype=I32) % BLOCK
    alive = (place_in.reshape(blocks, BLOCK) < valid_counts[:, None]).reshape(toks)
    marks = owner[:, None] == jnp.arange(32, dtype=I32)[None, :]
    marks3 = marks.astype(BF16).reshape(blocks, BLOCK, 32)
    tri = (jnp.arange(BLOCK)[:, None] > jnp.arange(BLOCK)[None, :]).astype(BF16)
    ahead = jnp.einsum("ij,bjk->bik", tri, marks3, preferred_element_type=F32)
    totals = jnp.sum(marks3.astype(F32), axis=1)
    tri_b = jnp.arange(blocks)[:, None] > jnp.arange(blocks)[None, :]
    base = jnp.sum(jnp.where(tri_b[:, :, None], totals[None], 0.0), axis=1)
    rank = jnp.sum(
        jnp.where(marks.reshape(blocks, BLOCK, 32), ahead + base[:, None, :], 0.0), axis=2
    )
    rank = rank.reshape(toks).astype(I32)
    fill = jnp.sum(totals, axis=0).astype(I32)
    target = owner * CAP + rank
    slot_marks = (rank[:, None] == jnp.arange(CAP, dtype=I32)[None, :]).astype(BF16)
    parts = jnp.stack([alive.astype(I32), within // 32, within % 32])
    parts = jnp.where(alive[None], parts, 0).astype(BF16)
    weights = parts[:, None, :] * marks.T.astype(BF16)[None]
    table = jnp.dot(
        weights.reshape(96, toks), slot_marks, preferred_element_type=F32
    ).reshape(3, 32, CAP)
    labels = jnp.where(table[0] > 0.5, table[1] * 32 + table[2], -1.0).astype(I32)
    return target, fill, labels


ROWS = 512


def dispatch_kernel(tgt, fill, counts, g_ref, v_ref, gain_ref, out_ref, rows, slots):
    step = pl.program_id(0)
    n_in = 4096 // ROWS
    plane = slots.shape[0] // 6

    @pl.when(step < n_in)
    def _():
        gain = gain_ref[...]
        for sub in range(ROWS // BLOCK):
            here = pl.ds(sub * BLOCK, BLOCK)
            x = v_ref[here, :].astype(F32)
            mu = jnp.mean(x, axis=1, keepdims=True)
            cen = x - mu
            inv = lax.rsqrt(jnp.mean(cen * cen, axis=1, keepdims=True) + 1e-12)
            scaled = gain * g_ref[here, :].astype(F32)
            first = jnp.mean(scaled, axis=1, keepdims=True)
            xhat = cen * inv
            second = jnp.mean(scaled * xhat, axis=1, keepdims=True)
            dx = inv * (scaled - first - xhat * second)
            live = lax.broadcasted_iota(I32, (BLOCK, 1), 0) < counts[step * (ROWS // BLOCK) + sub]
            dx = jnp.where(live, dx, 0.0)
            for j in range(6):
                rows[pl.ds(j * ROWS + sub * BLOCK, BLOCK), :] = dx[:, j * 128 : (j + 1) * 128]

        def body(i, carry):
            for u in range(8):
                t = tgt[step * ROWS + i * 8 + u]
                row = rows[pl.ds(i * 8 + u, 6, stride=ROWS), :]
                slots[pl.ds(t, 6, stride=plane), :] = row
            return carry

        lax.fori_loop(0, ROWS // 8, body, 0)

    @pl.when(step >= n_in)
    def _():
        at = step - n_in
        for k in range(4):
            filled = lax.broadcasted_iota(I32, (CAP, 1), 0) < fill[at * 4 + k]
            for j in range(6):
                part = slots[pl.ds(j * plane + (at * 4 + k) * CAP, CAP), :]
                out_ref[j // 2, pl.ds(k * CAP, CAP), pl.ds((j % 2) * 128, 128)] = jnp.where(
                    filled, part, 0.0
                ).astype(BF16)


def dispatch(target, fill, counts, grads, values, gain):
    n_in = 4096 // ROWS
    return pl.pallas_call(
        dispatch_kernel,
        out_shape=jax.ShapeDtypeStruct((3, 32 * CAP, 256), BF16),
        grid_spec=pltpu.PrefetchScalarGridSpec(
            num_scalar_prefetch=3,
            grid=(n_in + 8,),
            in_specs=[
                pl.BlockSpec((ROWS, 768), lambda i, *_: (jnp.minimum(i, n_in - 1), 0)),
                pl.BlockSpec((ROWS, 768), lambda i, *_: (jnp.minimum(i, n_in - 1), 0)),
                pl.BlockSpec((1, 768), lambda i, *_: (0, 0)),
            ],
            out_specs=pl.BlockSpec((3, 4 * CAP, 256), lambda i, *_: (0, jnp.maximum(i - n_in, 0), 0)),
            scratch_shapes=[
                pltpu.VMEM((6 * ROWS, 128), F32),
                pltpu.VMEM((6 * (32 * CAP + 8), 128), F32),
            ],
        ),
        compiler_params=pltpu.CompilerParams(vmem_limit_bytes=48 << 20),
        name="dispatch",
    )(target, fill, counts, grads, values, gain.reshape(1, 768))


ROW_AXES = ("z", "y", "x")


def exchange_kernel(box, lab, inbox, inlab, ss, rs, lss, lrs, own):
    x, z, y, c = place()
    barrier = pltpu.get_barrier_semaphore()
    hops = [(a, d, dc) for a in ROW_AXES for d in (1, 2, 3) for dc in (0, 1)] + [("x", 0, 1)]
    for a, d, dc in hops:
        pl.semaphore_signal(barrier, 1, device_id=shifted(a, d, dc), device_id_type=MESH)
    pl.semaphore_wait(barrier, len(hops))
    copies = []
    for d in (2, 1, 3, 0):
        for dc in (0, 1):
            for ch, a in enumerate(ROW_AXES):
                me = coordinate(a)
                q = (me + d) % 4
                cq = (c + dc) % 2
                for src, dst, s, r in ((box, inbox, ss, rs), (lab, inlab, lss, lrs)):
                    if src is box:
                        piece = box.at[ch, :, q, cq] if a == "y" else box.at[ch, q, :, cq]
                    else:
                        piece = lab.at[:, q, cq] if a == "y" else lab.at[q, :, cq]
                    if d == 0 and dc == 0:
                        copy = pltpu.make_async_copy(
                            piece, dst.at[ch, me, c], own.at[ch, 0 if src is box else 1]
                        )
                    else:
                        copy = pltpu.make_async_remote_copy(
                            src_ref=piece,
                            dst_ref=dst.at[ch, me, c],
                            send_sem=s.at[ch, d, dc],
                            recv_sem=r.at[ch, d, dc],
                            device_id=shifted(a, d, dc),
                            device_id_type=MESH,
                        )
                    copy.start()
                    copies.append(copy)
    for copy in copies:
        copy.wait()


def exchange(outbox, labels):
    any_space = pl.BlockSpec(memory_space=pl.ANY)
    return pl.pallas_call(
        exchange_kernel,
        out_shape=(
            jax.ShapeDtypeStruct((3, 4, 2, 4, CAP, 256), BF16),
            jax.ShapeDtypeStruct((3, 4, 2, 4, 2, 128), I32),
        ),
        in_specs=[any_space] * 2,
        out_specs=(any_space, any_space),
        scratch_shapes=[pltpu.SemaphoreType.DMA((3, 4, 2))] * 4 + [pltpu.SemaphoreType.DMA((3, 2))],
        compiler_params=pltpu.CompilerParams(collective_id=0, has_side_effects=True),
        name="exchange",
    )(outbox.reshape(3, 4, 4, 2, CAP, 256), labels.reshape(4, 4, 2, 2, 128))


def combine_kernel(in_ref, lab_ref, out_ref, picks):
    for s in range(8):
        for h in range(2):
            lab = lab_ref[0, s // 2, s % 2, 0, pl.ds(h, 1), :]
            hit = lax.broadcasted_iota(I32, (VOCAB_DEV, 128), 0) == lab
            picks[:, pl.ds(s * 256 + h * 128, 128)] = jnp.where(hit, 1.0, 0.0).astype(BF16)
    rows = in_ref[0, :, :, 0].reshape(2048, 256)
    for m in range(4):
        here = pl.ds(m * QROWS, QROWS)
        out_ref[0, 0, here, :] = jnp.dot(
            picks[here, :], rows, preferred_element_type=F32
        ).astype(BF16)


def combine(inbox, inlab):
    return pl.pallas_call(
        combine_kernel,
        grid=(3, 4),
        out_shape=jax.ShapeDtypeStruct((3, 4, VOCAB_DEV, 256), BF16),
        in_specs=[
            pl.BlockSpec((1, 4, 2, 1, CAP, 256), lambda i, k: (i, 0, 0, k, 0, 0)),
            pl.BlockSpec((1, 4, 2, 1, 2, 128), lambda i, k: (i, 0, 0, k, 0, 0)),
        ],
        out_specs=pl.BlockSpec((1, 1, VOCAB_DEV, 256), lambda i, k: (i, k, 0, 0)),
        scratch_shapes=[pltpu.VMEM((VOCAB_DEV, 2048), BF16)],
        name="combine",
    )(inbox, inlab)


def reduce_kernel(tab, out, got2a, got2, u, ub, got3, f, s2, r2, s3, r3, s4, r4, own):
    x, z, y, c = place()
    barrier = pltpu.get_barrier_semaphore()
    hops = [(a, d) for a in ("x", "y", "z") for d in (1, 2, 3)]
    for a, d in hops:
        pl.semaphore_signal(barrier, 1, device_id=shifted(a, d), device_id_type=MESH)
    for e in range(4):
        pl.semaphore_signal(
            barrier, 1, device_id=device((z + 0 * e), (e + 0 * z), y, c), device_id_type=MESH
        )
    pl.semaphore_wait(barrier, len(hops) + 4)

    first, second = ("x", "z", "y"), ("y", "x", "z")

    def send2(ch, d):
        q = (coordinate(first[ch]) + d) % 4
        if ch == 0:
            src, dst = tab.at[0, :, pl.ds(pl.multiple_of(q * QROWS, 16), QROWS)], got2a.at[d - 1]
        else:
            src, dst = tab.at[ch, q], got2.at[ch - 1, d - 1]
        return pltpu.make_async_remote_copy(
            src_ref=src, dst_ref=dst, send_sem=s2.at[ch, d - 1], recv_sem=r2.at[ch, d - 1],
            device_id=shifted(first[ch], d), device_id_type=MESH,
        )

    def send3(ch, d):
        q = (coordinate(second[ch]) + d) % 4
        return pltpu.make_async_remote_copy(
            src_ref=ub.at[ch, q], dst_ref=got3.at[ch, d - 1],
            send_sem=s3.at[ch, d - 1], recv_sem=r3.at[ch, d - 1],
            device_id=shifted(second[ch], d), device_id_type=MESH,
        )

    def send4(ch, d):
        dst = out.at[pl.ds(pl.multiple_of(x * QROWS, 16), QROWS), pl.ds(ch * 256, 256)]
        return pltpu.make_async_remote_copy(
            src_ref=f.at[ch], dst_ref=dst, send_sem=s4.at[ch, d], recv_sem=r4.at[ch, d],
            device_id=shifted("x", d), device_id_type=MESH,
        )

    twos = {(ch, d): send2(ch, d) for d in (2, 1, 3) for ch in range(3)}
    for copy in twos.values():
        copy.start()
    threes = {}
    for ch in range(3):
        for d in (1, 2, 3):
            twos[ch, d].wait()
        me = coordinate(first[ch])
        for p in range(4):
            at = pl.ds(p * QROWS, QROWS)
            if ch == 0:
                mine = tab[0, p, pl.ds(pl.multiple_of(me * QROWS, 16), QROWS), :].astype(F32)
                for d in range(3):
                    mine += got2a[d, p].astype(F32)
            else:
                mine = tab[ch, me, at, :].astype(F32)
                for d in range(3):
                    mine += got2[ch - 1, d, at, :].astype(F32)
            u[ch, p] = mine
            ub[ch, p] = mine.astype(BF16)
        for d in (2, 1, 3):
            threes[ch, d] = send3(ch, d)
            threes[ch, d].start()
    fours = []
    for ch in range(3):
        for d in (1, 2, 3):
            threes[ch, d].wait()
        me = coordinate(second[ch])
        total = u[ch, me]
        for d in range(3):
            total += got3[ch, d].astype(F32)
        f[ch] = total.astype(BF16)
        if ch < 2:
            out[pl.ds(pl.multiple_of(x * QROWS, 16), QROWS), pl.ds(ch * 256, 256)] = f[ch]
            for d in (2, 1, 3):
                copy = send4(ch, d)
                copy.start()
                fours.append(copy)
    rows = pl.ds(pl.multiple_of(z * QROWS, 16), QROWS)

    def send5(e):
        return pltpu.make_async_remote_copy(
            src_ref=f.at[2], dst_ref=out.at[rows, pl.ds(512, 256)],
            send_sem=s4.at[2, e], recv_sem=r4.at[2, z],
            device_id=device((x + e) % 4, x, y, c), device_id_type=MESH,
        )

    @pl.when(x == z)
    def _():
        out[rows, pl.ds(512, 256)] = f[2]

    for e in range(4):
        if e == 0:

            @pl.when(x != z)
            def _():
                send5(0).start()
        else:
            send5(e).start()
    for e in range(4):
        if e == 0:

            @pl.when(x != z)
            def _():
                send5(0).wait_send()
        else:
            send5(e).wait_send()
    for q in range(4):

        @pl.when(jnp.logical_or(x != z, q != z))
        def _():
            pltpu.make_async_remote_copy(
                src_ref=f.at[2], dst_ref=out.at[pl.ds(q * QROWS, QROWS), pl.ds(512, 256)],
                send_sem=s4.at[2, 0], recv_sem=r4.at[2, q],
                device_id=device(x, z, y, c), device_id_type=MESH,
            ).wait_recv()

    for copy in fours:
        copy.wait()


def reduce_tables(tables):
    vmem = pl.BlockSpec(memory_space=pltpu.VMEM)
    return pl.pallas_call(
        reduce_kernel,
        out_shape=jax.ShapeDtypeStruct((VOCAB_DEV, 768), BF16),
        in_specs=[vmem],
        out_specs=vmem,
        scratch_shapes=[
            pltpu.VMEM((3, 4, QROWS, 256), BF16),
            pltpu.VMEM((2, 3, VOCAB_DEV, 256), BF16),
            pltpu.VMEM((3, 4, QROWS, 256), F32),
            pltpu.VMEM((3, 4, QROWS, 256), BF16),
            pltpu.VMEM((3, 3, QROWS, 256), BF16),
            pltpu.VMEM((3, QROWS, 256), BF16),
            pltpu.SemaphoreType.DMA((3, 3)),
            pltpu.SemaphoreType.DMA((3, 3)),
            pltpu.SemaphoreType.DMA((3, 3)),
            pltpu.SemaphoreType.DMA((3, 3)),
            pltpu.SemaphoreType.DMA((3, 4)),
            pltpu.SemaphoreType.DMA((3, 4)),
            pltpu.SemaphoreType.DMA((1,)),
        ],
        compiler_params=pltpu.CompilerParams(collective_id=1, has_side_effects=True),
        name="reduce_tables",
    )(tables)


def per_device(token_ids, valid_counts, grad_output, pre_norm, norm_gain):
    target, fill, labels = routing(token_ids, valid_counts)
    outbox = dispatch(target, fill, valid_counts, grad_output, pre_norm, norm_gain)
    inbox, inlab = exchange(outbox, labels)
    tables = combine(inbox, inlab)
    return reduce_tables(tables).astype(F32)


def solution(mesh):
    in_specs = (
        P(("dp", "vocab")),
        P(("dp", "vocab")),
        P(("dp", "vocab"), None),
        P(("dp", "vocab"), None),
        P(),
    )
    return jax.shard_map(
        per_device, mesh=mesh, in_specs=in_specs, out_specs=P("vocab", None), check_vma=False
    )
```

time: 331 us -> 173 us (0.52)
  Pallas kernels: 0 us -> 159 us
  blocking collectives: 148 us -> 0 us
  waiting for transfers between devices: 69.2 us -> 0 us
  other arithmetic: 54 us -> 6.15 us
  local copies, waits for them, and re-layouts: 20.5 us -> 2.7 us
  matrix products: 15.1 us -> 1.21 us
  between operations: 13.5 us -> 0.1 us
  starting transfers between devices: 8.56 us -> 0 us
    pallas_call x0 -> x4, Pallas kernels: none -> 159 us  [the longest x1 57.5 us: reduce_tables(): pl.pallas_call(reduce_kernel, out_shape=jax.ShapeDtypeStruct((VOCAB_DEV,...]
    all_to_all x1 -> x0, blocking collectives: 148 us -> none  [per_device(): lax.all_to_all(outbox, 'vocab', split_axis=0, concat_axis=0, tiled=True)]
    psum x1 -> x0, waiting for transfers between devices: 69.2 us -> none  [per_device(): table = lax.psum(partial_table, 'dp')]
    scatter x1 -> x0, other arithmetic: 28.5 us -> none  [per_device(): jnp.zeros((shards * per_owner, width), jnp.bfloat16).at[target].set(rows)]
    scatter x1 -> x0, local copies, waits for them, and re-layouts: 16.1 us -> none  [per_device(): jnp.full((shards * per_owner,), -1, jnp.int32).at[target]]
    dot_general x1 -> x2, matrix products: 15.1 us -> 1.21 us  [the longest x1 0.91 us: routing(): jnp.dot(weights.reshape(96, toks), slot_marks, preferred_element_type=F32)]
    reduce_sum x4 -> x2, other arithmetic: 14.3 us -> 0.5 us  [the longest x1 0.28 us: routing(): fill = jnp.sum(totals, axis=0).astype(I32)]
    another operation x2 -> x0, other arithmetic: 9.41 us -> none
  transfers between devices with their start and end apart: 2 -> 0, of which waited for: 1 -> 0; matrix products, arithmetic and copies ran while one was open for 13% -> 0% of each run, Pallas kernels for 0% -> 0%
where the time goes in v1:
time: 173 us; the launch traced here: 169 us
  Pallas kernels  159 us (92%)
  other arithmetic  6.15 us (4%)
  local copies, waits for them, and re-layouts  2.7 us (2%)
    pallas_call x1, Pallas kernels, reduce_tables(): pl.pallas_call(reduce_kernel, out_shape=jax.ShapeDtypeStruct((VOCAB_DEV,...  57.5 us
    pallas_call x1, Pallas kernels, exchange(): pl.pallas_call(exchange_kernel, out_shape=(jax.ShapeDtypeStruct((3, 4, 2,...  54.6 us
    pallas_call x1, Pallas kernels, dispatch(): pl.pallas_call(dispatch_kernel, out_shape=jax.ShapeDtypeStruct((3, 32 * C...  28.9 us
    pallas_call x1, Pallas kernels, combine(): pl.pallas_call(combine_kernel, grid=(3, 4), out_shape=jax.ShapeDtypeStruc...  18.3 us

profile of v1, /device:TPU:2, one launch (start us, length us, event | category | flops | bytes accessed | tf_op | source)
XLA Modules:
  0.0 169.4 jit_solution(15483937419228595611)
XLA Ops:
  0.0 0.7 reshape.172.gain_ref
  0.7 0.7 fusion.13
  1.4 0.7 fusion.20
  2.2 0.7 lt.40
  2.9 0.3 convert_reduce_fusion
  3.2 0.2 select_reduce_fusion
  3.4 0.3 fusion.4
  3.8 0.8 add_select_fusion.2
  4.5 0.1 fusion.8
  4.6 0.1 broadcast_multiply_fusion
  4.7 0.9 fusion
  5.7 0.6 convert_element_type.67.lab
  6.3 0.0 copy-start
  6.3 0.7 copy-done
  6.9 28.9 %dispatch.1 = bf16[3,8192,256]{2,1,0:T(8,128)(2,1)} custom-call(s32[4096]{0:T(1024)S(1)} %get-tuple-element.12.tgt, s32[32]{0:T(128)S(1)} %convert_element_type.62.fill, s32[32]{0:T(128)S(1)} %copy-done, bf16[4096,768]{1,0:T(8,128)(2,1)} %g_ref.1, bf16[4096,768]{1,0:T(8,128)(2,1)} %v_ref.1, f32[1,768]{1,0:T(1,128)S(1)} %reshape.172.gain_ref), custom_call_target="tpu_custom_call" | custom-call | tf_op jit(solution)/shard_map/dispatch/pallas_call | solution.py:124
  35.9 54.6 %exchange.1 = (bf16[3,4,2,4,256,256]{5,4,3,2,1,0:T(8,128)(2,1)}, s32[3,4,2,4,2,128]{5,4,3,2,1,0:T(2,128)}) custom-call(bf16[3,4,4,2,256,256]{5,4,3,2,1,0:T(8,128)(2,1)} %bitcast.23, s32[4,4,2,2,128]{4,3,2,1,0:T(2,128)} %convert_element_type.67.lab), custom_call_target="tpu_custom_call" | custom-call | tf_op jit(solution)/shard_map/exchange/pallas_call | solution.py:189
  90.4 18.3 %combine.1.tab = bf16[3,4,960,256]{3,2,1,0:T(8,128)(2,1)} custom-call(bf16[3,4,2,4,256,256]{5,4,3,2,1,0:T(8,128)(2,1)} %get-tuple-element.7.in_ref, s32[3,4,2,4,2,128]{5,4,3,2,1,0:T(2,128)} %get-tuple-element.8.lab_ref), custom_call_target="tpu_custom_call" | custom-call | tf_op jit(solution)/shard_map/combine/pallas_call | solution.py:218
  108.7 57.5 %reduce_tables.1 = bf16[960,768]{1,0:T(8,128)(2,1)} custom-call(bf16[3,4,960,256]{3,2,1,0:T(8,128)(2,1)} %combine.1.tab), custom_call_target="tpu_custom_call" | custom-call | tf_op jit(solution)/shard_map/reduce_tables/pallas_call | solution.py:355
  166.2 3.2 %convert_element_type.68 = f32[960,768]{1,0:T(8,128)} convert(bf16[960,768]{1,0:T(8,128)(2,1)} %reduce_tables.1) | non-fusion elementwise | flops 737280 | bytes 4423680 | tf_op jit(solution)/shard_map/convert_element_type | solution.py:385
  (6 shorter events, 0.1 us)
Async XLA Ops:
  6.3 0.7 copy-start

commit v2 on v1

v2 whole, which is shorter than its diff:
```python
import functools

import jax
import jax.numpy as jnp
from jax import lax
from jax.experimental import pallas as pl
from jax.experimental.pallas import tpu as pltpu
from jax.sharding import PartitionSpec as P

VOCAB_DEV = 960
BLOCK = 128
CAP = 256
QROWS = VOCAB_DEV // 4
MESH = pl.DeviceIdType.MESH
F32, BF16, I32 = jnp.float32, jnp.bfloat16, jnp.int32


def place():
    x = lax.axis_index("dp")
    v = lax.axis_index("vocab")
    return x, v // 8, (v // 2) % 4, v % 2


def device(x, z, y, c):
    return (x, z * 8 + y * 2 + c)


def shifted(axis, d, dc=0):
    x, z, y, c = place()
    c = (c + dc) % 2
    if axis == "x":
        return device((x + d) % 4, z, y, c)
    if axis == "y":
        return device(x, z, (y + d) % 4, c)
    return device(x, (z + d) % 4, y, c)


def coordinate(axis):
    x, z, y, _ = place()
    return {"x": x, "y": y, "z": z}[axis]


def routing(token_ids, valid_counts):
    toks = token_ids.shape[0]
    blocks = toks // BLOCK
    owner = token_ids // VOCAB_DEV
    within = token_ids - owner * VOCAB_DEV
    place_in = jnp.arange(toks, dtype=I32) % BLOCK
    alive = (place_in.reshape(blocks, BLOCK) < valid_counts[:, None]).reshape(toks)
    marks = owner[:, None] == jnp.arange(32, dtype=I32)[None, :]
    marks3 = marks.astype(BF16).reshape(blocks, BLOCK, 32)
    tri = (jnp.arange(BLOCK)[:, None] > jnp.arange(BLOCK)[None, :]).astype(BF16)
    ahead = jnp.einsum("ij,bjk->bik", tri, marks3, preferred_element_type=F32)
    totals = jnp.sum(marks3.astype(F32), axis=1)
    tri_b = jnp.arange(blocks)[:, None] > jnp.arange(blocks)[None, :]
    base = jnp.sum(jnp.where(tri_b[:, :, None], totals[None], 0.0), axis=1)
    rank = jnp.sum(
        jnp.where(marks.reshape(blocks, BLOCK, 32), ahead + base[:, None, :], 0.0), axis=2
    )
    rank = rank.reshape(toks).astype(I32)
    fill = jnp.sum(totals, axis=0).astype(I32)
    target = owner * CAP + rank
    slot_marks = (rank[:, None] == jnp.arange(CAP, dtype=I32)[None, :]).astype(BF16)
    parts = jnp.stack([alive.astype(I32), within // 32, within % 32])
    parts = jnp.where(alive[None], parts, 0).astype(BF16)
    weights = parts[:, None, :] * marks.T.astype(BF16)[None]
    table = jnp.dot(
        weights.reshape(96, toks), slot_marks, preferred_element_type=F32
    ).reshape(3, 32, CAP)
    labels = jnp.where(table[0] > 0.5, table[1] * 32 + table[2], -1.0).astype(I32)
    return target, fill, labels


ROWS = 512


def dispatch_kernel(tgt, fill, counts, g_ref, v_ref, gain_ref, out_ref, rows, slots):
    step = pl.program_id(0)
    n_in = 4096 // ROWS
    plane = slots.shape[0] // 6

    @pl.when(step < n_in)
    def _():
        gain = gain_ref[...]
        for sub in range(ROWS // BLOCK):
            here = pl.ds(sub * BLOCK, BLOCK)
            x = v_ref[here, :].astype(F32)
            mu = jnp.mean(x, axis=1, keepdims=True)
            cen = x - mu
            inv = lax.rsqrt(jnp.mean(cen * cen, axis=1, keepdims=True) + 1e-12)
            scaled = gain * g_ref[here, :].astype(F32)
            first = jnp.mean(scaled, axis=1, keepdims=True)
            xhat = cen * inv
            second = jnp.mean(scaled * xhat, axis=1, keepdims=True)
            dx = inv * (scaled - first - xhat * second)
            live = lax.broadcasted_iota(I32, (BLOCK, 1), 0) < counts[step * (ROWS // BLOCK) + sub]
            dx = jnp.where(live, dx, 0.0)
            for j in range(6):
                rows[pl.ds(j * (ROWS + 8) + sub * BLOCK, BLOCK), :] = dx[:, j * 128 : (j + 1) * 128]

        def body(i, carry):
            for u in range(16):
                t = tgt[step * ROWS + i * 16 + u]
                row = rows[pl.ds(i * 16 + u, 6, stride=ROWS + 8), :]
                slots[pl.ds(t, 6, stride=plane), :] = row
            return carry

        lax.fori_loop(0, ROWS // 16, body, 0)

    @pl.when(step >= n_in)
    def _():
        at = step - n_in
        for k in range(4):
            filled = lax.broadcasted_iota(I32, (CAP, 1), 0) < fill[at * 4 + k]
            for j in range(6):
                part = slots[pl.ds(j * plane + (at * 4 + k) * CAP, CAP), :]
                out_ref[j // 2, pl.ds(k * CAP, CAP), pl.ds((j % 2) * 128, 128)] = jnp.where(
                    filled, part, 0.0
                ).astype(BF16)


def dispatch(target, fill, counts, grads, values, gain):
    n_in = 4096 // ROWS
    return pl.pallas_call(
        dispatch_kernel,
        out_shape=jax.ShapeDtypeStruct((3, 32 * CAP, 256), BF16),
        grid_spec=pltpu.PrefetchScalarGridSpec(
            num_scalar_prefetch=3,
            grid=(n_in + 8,),
            in_specs=[
                pl.BlockSpec((ROWS, 768), lambda i, *_: (jnp.minimum(i, n_in - 1), 0)),
                pl.BlockSpec((ROWS, 768), lambda i, *_: (jnp.minimum(i, n_in - 1), 0)),
                pl.BlockSpec((1, 768), lambda i, *_: (0, 0)),
            ],
            out_specs=pl.BlockSpec((3, 4 * CAP, 256), lambda i, *_: (0, jnp.maximum(i - n_in, 0), 0)),
            scratch_shapes=[
                pltpu.VMEM((6 * (ROWS + 8), 128), F32),
                pltpu.VMEM((6 * (32 * CAP + 8), 128), F32),
            ],
        ),
        compiler_params=pltpu.CompilerParams(vmem_limit_bytes=48 << 20),
        name="dispatch",
    )(target, fill, counts, grads, values, gain.reshape(1, 768))


ROW_AXES = ("z", "y", "x")
FIRST = ("x", "z", "y")
SECOND = ("y", "x", "z")
STEPS = (2, 1, 3, 0)


def quarter(ref, q):
    return ref.at[pl.ds(pl.multiple_of(q * QROWS, 16), QROWS)]


def table_kernel(
    box, lab, out, inbox, inlab, tab, got2a, got2, u0, u1, ub0, ub1, got3, f,
    s1, r1, sl, rl, own1, s2a, r2a, s2, r2, s3, r3, s4, r4,
):
    x, z, y, c = place()
    barrier = pltpu.get_barrier_semaphore()
    hops = [(a, d, dc) for a in ROW_AXES for d in (1, 2, 3) for dc in (0, 1)] + [("x", 0, 1)]
    for a, d, dc in hops:
        pl.semaphore_signal(barrier, 1, device_id=shifted(a, d, dc), device_id_type=MESH)
    for e in range(4):
        pl.semaphore_signal(barrier, 1, device_id=device(z, e, y, c), device_id_type=MESH)
    pl.semaphore_wait(barrier, len(hops) + 4)

    def remote(src, dst, send, recv, to):
        return pltpu.make_async_remote_copy(
            src_ref=src, dst_ref=dst, send_sem=send, recv_sem=recv, device_id=to, device_id_type=MESH
        )

    def owner_of(ch, r):
        return ((z if ch == 1 else y) + r) % 4

    def row_copy(ch, r, d, dc):
        q = (coordinate(ROW_AXES[ch]) + d) % 4
        w = owner_of(ch, r)
        cq = (c + dc) % 2
        src = box.at[ch, w, q, cq] if ch == 1 else box.at[ch, q, w, cq]
        k = d * 2 + dc
        if k == 0:
            return pltpu.make_async_copy(src, inbox.at[ch, r, 0], own1.at[ch, r])
        return remote(
            src, inbox.at[ch, r, k], s1.at[ch, r, k], r1.at[ch, r, k], shifted(ROW_AXES[ch], d, dc)
        )

    def label_copy(ch, d, dc):
        q = (coordinate(ROW_AXES[ch]) + d) % 4
        cq = (c + dc) % 2
        src = lab.at[:, q, cq] if ch == 1 else lab.at[q, :, cq]
        k = d * 2 + dc
        if k == 0:
            return pltpu.make_async_copy(src, inlab.at[ch, 0], own1.at[ch, 4])
        return remote(src, inlab.at[ch, k], sl.at[ch, k], rl.at[ch, k], shifted(ROW_AXES[ch], d, dc))

    routes = [(d, dc) for d in (2, 1, 3, 0) for dc in (0, 1)]
    labels = {}
    rows = {}
    for d, dc in routes:
        for ch in range(3):
            labels[ch, d, dc] = label_copy(ch, d, dc)
            labels[ch, d, dc].start()
    for r in STEPS:
        for d, dc in routes:
            for ch in range(3):
                rows[ch, r, d, dc] = row_copy(ch, r, d, dc)
                rows[ch, r, d, dc].start()

    def arrived(copy, local):
        if local:
            copy.wait()
        else:
            copy.wait_recv()

    twos = {}
    for r in STEPS:
        for ch in range(3):
            for d, dc in routes:
                if r == STEPS[0]:
                    arrived(labels[ch, d, dc], d + dc == 0)
                arrived(rows[ch, r, d, dc], d + dc == 0)
            w = owner_of(ch, r)

            def part(m, carry):
                ids = lax.broadcasted_iota(I32, (QROWS, 128), 0) + m * QROWS
                total = None
                for k in range(8):
                    picks = jnp.concatenate(
                        [
                            jnp.where(ids == inlab[ch, k, w, pl.ds(h, 1), :], 1.0, 0.0).astype(BF16)
                            for h in range(2)
                        ],
                        axis=1,
                    )
                    add = jnp.dot(picks, inbox[ch, r, k], preferred_element_type=F32)
                    total = add if total is None else total + add
                at = pl.ds(pl.multiple_of(m * QROWS, 16), QROWS)
                if ch > 0 and r == 0:
                    u1[ch - 1, at, :] = total
                else:
                    tab[ch, r, at, :] = total.astype(BF16)
                if ch == 0:

                    @pl.when(m == x)
                    def _():
                        u0[r] = total

                return carry

            lax.fori_loop(0, 4, part, 0)
            if ch == 0:
                for d in (2, 1, 3):
                    twos[0, r, d] = remote(
                        quarter(tab.at[0, r], (x + d) % 4), got2a.at[r, d - 1],
                        s2a.at[r, d - 1], r2a.at[r, d - 1], shifted("x", d),
                    )
                    twos[0, r, d].start()
            elif r > 0:
                twos[ch, r] = remote(
                    tab.at[ch, r], got2.at[ch - 1, r - 1],
                    s2.at[ch - 1, r - 1], r2.at[ch - 1, r - 1], shifted(FIRST[ch], r),
                )
                twos[ch, r].start()

    threes = {}
    for r in STEPS:
        for d in (2, 1, 3):
            twos[0, r, d].wait_recv()
        total = u0[r]
        for d in range(3):
            total += got2a[r, d].astype(F32)
        if r == 0:
            u0[0] = total
        else:
            ub0[r - 1] = total.astype(BF16)
            threes[0, r] = remote(
                ub0.at[r - 1], got3.at[0, r - 1], s3.at[0, r - 1], r3.at[0, r - 1], shifted("y", r)
            )
            threes[0, r].start()
    for ch in (1, 2):
        for r in (2, 1, 3):
            twos[ch, r].wait_recv()
        me = coordinate(SECOND[ch])
        for d in (2, 1, 3, 0):
            at = pl.ds(pl.multiple_of((me + d) % 4 * QROWS, 16), QROWS)
            total = u1[ch - 1, at, :]
            for e in range(3):
                total += got2[ch - 1, e, at, :].astype(F32)
            if d == 0:
                u1[ch - 1, at, :] = total
            else:
                ub1[ch - 1, d - 1] = total.astype(BF16)
                threes[ch, d] = remote(
                    ub1.at[ch - 1, d - 1], got3.at[ch, d - 1],
                    s3.at[ch, d - 1], r3.at[ch, d - 1], shifted(SECOND[ch], d),
                )
                threes[ch, d].start()

    fours = []
    for ch in range(3):
        for d in (2, 1, 3):
            threes[ch, d].wait_recv()
        if ch == 0:
            total = u0[0]
        else:
            me = coordinate(SECOND[ch])
            total = u1[ch - 1, pl.ds(pl.multiple_of(me * QROWS, 16), QROWS), :]
        for d in range(3):
            total += got3[ch, d].astype(F32)
        f[ch] = total.astype(BF16)
        if ch < 2:
            mine = out.at[pl.ds(pl.multiple_of(x * QROWS, 16), QROWS), pl.ds(ch * 256, 256)]
            mine[...] = f[ch]
            for d in (2, 1, 3):
                copy = remote(f.at[ch], mine, s4.at[ch, d], r4.at[ch, d], shifted("x", d))
                copy.start()
                fours.append(copy)

    mine = out.at[pl.ds(pl.multiple_of(z * QROWS, 16), QROWS), pl.ds(512, 256)]

    def last(e):
        return remote(f.at[2], mine, s4.at[2, e], r4.at[2, z], device((x + e) % 4, x, y, c))

    @pl.when(x == z)
    def _():
        mine[...] = f[2]

    @pl.when(x != z)
    def _():
        last(0).start()

    for e in (2, 1, 3):
        last(e).start()
    for q in range(4):

        @pl.when(jnp.logical_or(x != z, q != z))
        def _():
            remote(
                f.at[2], out.at[pl.ds(q * QROWS, QROWS), pl.ds(512, 256)],
                s4.at[2, 0], r4.at[2, q], device(x, z, y, c),
            ).wait_recv()

    for copy in fours:
        copy.wait()

    @pl.when(x != z)
    def _():
        last(0).wait_send()

    for e in (2, 1, 3):
        last(e).wait_send()
    for ch, d, dc in labels:
        if d + dc:
            labels[ch, d, dc].wait_send()
    for ch, r, d, dc in rows:
        if d + dc:
            rows[ch, r, d, dc].wait_send()
    for copy in list(twos.values()) + list(threes.values()):
        copy.wait_send()


def table_sums(outbox, labels):
    any_space = pl.BlockSpec(memory_space=pl.ANY)
    dma = pltpu.SemaphoreType.DMA
    return pl.pallas_call(
        table_kernel,
        out_shape=jax.ShapeDtypeStruct((VOCAB_DEV, 768), BF16),
        in_specs=[any_space] * 2,
        out_specs=pl.BlockSpec(memory_space=pltpu.VMEM),
        scratch_shapes=[
            pltpu.VMEM((3, 4, 8, CAP, 256), BF16),
            pltpu.VMEM((3, 8, 4, 2, 128), I32),
            pltpu.VMEM((3, 4, VOCAB_DEV, 256), BF16),
            pltpu.VMEM((4, 3, QROWS, 256), BF16),
            pltpu.VMEM((2, 3, VOCAB_DEV, 256), BF16),
            pltpu.VMEM((4, QROWS, 256), F32),
            pltpu.VMEM((2, VOCAB_DEV, 256), F32),
            pltpu.VMEM((3, QROWS, 256), BF16),
            pltpu.VMEM((2, 3, QROWS, 256), BF16),
            pltpu.VMEM((3, 3, QROWS, 256), BF16),
            pltpu.VMEM((3, QROWS, 256), BF16),
            dma((3, 4, 8)),
            dma((3, 4, 8)),
            dma((3, 8)),
            dma((3, 8)),
            dma((3, 5)),
            dma((4, 3)),
            dma((4, 3)),
            dma((2, 3)),
            dma((2, 3)),
            dma((3, 3)),
            dma((3, 3)),
            dma((3, 4)),
            dma((3, 4)),
        ],
        compiler_params=pltpu.CompilerParams(
            collective_id=0, has_side_effects=True, vmem_limit_bytes=56 << 20
        ),
        name="table_sums",
    )(outbox.reshape(3, 4, 4, 2, CAP, 256), labels.reshape(4, 4, 2, 2, 128))


def per_device(token_ids, valid_counts, grad_output, pre_norm, norm_gain):
    target, fill, labels = routing(token_ids, valid_counts)
    outbox = dispatch(target, fill, valid_counts, grad_output, pre_norm, norm_gain)
    return table_sums(outbox, labels).astype(F32)


def solution(mesh):
    in_specs = (
        P(("dp", "vocab")),
        P(("dp", "vocab")),
        P(("dp", "vocab"), None),
        P(("dp", "vocab"), None),
        P(),
    )
    return jax.shard_map(
        per_device, mesh=mesh, in_specs=in_specs, out_specs=P("vocab", None), check_vma=False
    )
```

time: 173 us -> 139 us (0.80); the launches traced: 169 us -> 139 us
  Pallas kernels: 159 us -> 129 us
    pallas_call x3 -> x1, Pallas kernels: 130 us -> 106 us  [table_sums(): pl.pallas_call(table_kernel, out_shape=jax.ShapeDtypeStruct((VOCAB_DEV, 7...]
    pallas_call x1, Pallas kernels: 28.9 us -> 23.1 us  [dispatch(): pl.pallas_call(dispatch_kernel, out_shape=jax.ShapeDtypeStruct((3, 32 * C...]
where the time goes in v2:
time: 139 us
  Pallas kernels  129 us (93%)
  other arithmetic  6.15 us (4%)
  local copies, waits for them, and re-layouts  2.07 us (1%)
    pallas_call x1, Pallas kernels, table_sums(): pl.pallas_call(table_kernel, out_shape=jax.ShapeDtypeStruct((VOCAB_DEV, 7...  106 us
    pallas_call x1, Pallas kernels, dispatch(): pl.pallas_call(dispatch_kernel, out_shape=jax.ShapeDtypeStruct((3, 32 * C...  23.1 us
    convert_element_type x1, other arithmetic, per_device(): return table_sums(outbox, labels).astype(F32)  3.19 us

profile of v2, /device:TPU:2, one launch (start us, length us, event | category | flops | bytes accessed | tf_op | source)
XLA Modules:
  0.0 138.5 jit_solution(14535491562317530196)
XLA Ops:
  0.0 0.0 copy-start
  0.0 0.7 reshape.172.gain_ref
  0.7 0.7 fusion.13
  1.4 0.7 fusion.20
  2.2 0.7 lt.40
  2.9 0.3 convert_reduce_fusion
  3.2 0.2 select_reduce_fusion
  3.5 0.3 fusion.4
  3.8 0.8 add_select_fusion.2
  4.5 0.1 fusion.8
  4.7 0.1 broadcast_multiply_fusion
  4.7 0.9 fusion
  5.7 0.6 convert_element_type.67.lab
  6.3 0.0 copy-done
  6.3 23.1 %dispatch.1 = bf16[3,8192,256]{2,1,0:T(8,128)(2,1)} custom-call(s32[4096]{0:T(1024)S(1)} %get-tuple-element.8.tgt, s32[32]{0:T(128)S(1)} %convert_element_type.62.fill, s32[32]{0:T(128)S(1)} %copy-done, bf16[4096,768]{1,0:T(8,128)(2,1)} %g_ref.1, bf16[4096,768]{1,0:T(8,128)(2,1)} %v_ref.1, f32[1,768]{1,0:T(1,128)S(1)} %reshape.172.gain_ref), custom_call_target="tpu_custom_call" | custom-call | tf_op jit(solution)/shard_map/dispatch/pallas_call | solution.py:124
  29.4 105.9 %table_sums.1 = bf16[960,768]{1,0:T(8,128)(2,1)} custom-call(bf16[3,4,4,2,256,256]{5,4,3,2,1,0:T(8,128)(2,1)} %bitcast.23, s32[4,4,2,2,128]{4,3,2,1,0:T(2,128)} %convert_element_type.67.lab), custom_call_target="tpu_custom_call" | custom-call | tf_op jit(solution)/shard_map/table_sums/pallas_call | solution.py:367
  135.3 3.2 %convert_element_type.68 = f32[960,768]{1,0:T(8,128)} convert(bf16[960,768]{1,0:T(8,128)(2,1)} %table_sums.1) | non-fusion elementwise | flops 737280 | bytes 4423680 | tf_op jit(solution)/shard_map/convert_element_type | solution.py:408
  (6 shorter events, 0.1 us)
Async XLA Ops:
  0.0 6.3 %copy-start = (s32[32]{0:T(128)S(1)}, s32[32]{0:T(128)}, u32[]{:S(2)}) copy-start(s32[32]{0:T(128)} %counts.1) | copy-start | bytes 388

commit v3 on v2

v3 whole, which is shorter than its diff:
```python
import functools

import jax
import jax.numpy as jnp
from jax import lax
from jax.experimental import pallas as pl
from jax.experimental.pallas import tpu as pltpu
from jax.sharding import PartitionSpec as P

VOCAB_DEV = 960
BLOCK = 128
CAP = 256
QROWS = VOCAB_DEV // 4
MESH = pl.DeviceIdType.MESH
F32, BF16, I32 = jnp.float32, jnp.bfloat16, jnp.int32


def place():
    x = lax.axis_index("dp")
    v = lax.axis_index("vocab")
    return x, v // 8, (v // 2) % 4, v % 2


def device(x, z, y, c):
    return (x, z * 8 + y * 2 + c)


def shifted(axis, d, dc=0):
    x, z, y, c = place()
    c = (c + dc) % 2
    if axis == "x":
        return device((x + d) % 4, z, y, c)
    if axis == "y":
        return device(x, z, (y + d) % 4, c)
    return device(x, (z + d) % 4, y, c)


def coordinate(axis):
    x, z, y, _ = place()
    return {"x": x, "y": y, "z": z}[axis]


TOKS = 4096
BLOCKS = TOKS // BLOCK


def routing_kernel(counts, ids_ref, tok_ref, lab_ref, weights, slots):
    owner_row = lax.broadcasted_iota(I32, (32, BLOCK), 0)
    lane = lax.broadcasted_iota(I32, (1, BLOCK), 1)
    ids = ids_ref[...]
    owner = lax.shift_right_logical(ids * 34953, 25)
    within = ids - owner * VOCAB_DEV
    before = (
        lax.broadcasted_iota(I32, (BLOCK, BLOCK), 0) < lax.broadcasted_iota(I32, (BLOCK, BLOCK), 1)
    )
    before = jnp.where(before, 1.0, 0.0).astype(BF16)
    base = jnp.zeros((32, 1), F32)
    slot_row = lax.broadcasted_iota(I32, (CAP, BLOCK), 0)
    for b in range(BLOCKS):
        mark = owner_row == owner[b : b + 1]
        ones = jnp.where(mark, 1.0, 0.0)
        ahead = jnp.dot(ones.astype(BF16), before, preferred_element_type=F32)
        rank = jnp.sum(jnp.where(mark, ahead + base, 0.0), axis=0, keepdims=True).astype(I32)
        base = base + jnp.sum(ones, axis=1, keepdims=True)
        live = lane < counts[b]
        mark = jnp.logical_and(mark, live)
        off = within[b : b + 1]
        at = pl.ds(b * BLOCK, BLOCK)
        for p, value in enumerate(
            (
                jnp.ones((1, BLOCK), F32),
                lax.shift_right_logical(off, 5).astype(F32),
                (off & 31).astype(F32),
                (b * 2 + lax.shift_right_logical(lane, 6)).astype(F32),
                (lane & 63).astype(F32),
            )
        ):
            weights[pl.ds(p * 32, 32), at] = jnp.where(mark, value, 0.0).astype(BF16)
        slots[:, at] = jnp.where(slot_row == rank, 1.0, 0.0).astype(BF16)
    table = lax.dot_general(
        weights[...], slots[...], (((1,), (1,)), ((), ())), preferred_element_type=F32
    )
    used, high, low, block, place_in = (table[p * 32 : (p + 1) * 32] for p in range(5))
    labels = jnp.where(used > 0.5, high * 32.0 + low, -1.0).astype(I32)
    for h in range(2):
        lab_ref[:, h, :] = labels[:, h * 128 : (h + 1) * 128]
    tok_ref[...] = jnp.where(used > 0.5, block * 64.0 + place_in, float(TOKS)).astype(I32)


def routing(token_ids, valid_counts):
    return pl.pallas_call(
        routing_kernel,
        grid_spec=pltpu.PrefetchScalarGridSpec(
            num_scalar_prefetch=1,
            grid=(1,),
            in_specs=[pl.BlockSpec((BLOCKS, BLOCK), lambda i, _: (0, 0))],
            out_specs=[
                pl.BlockSpec((32, CAP), lambda i, _: (0, 0)),
                pl.BlockSpec((32, 2, 128), lambda i, _: (0, 0, 0)),
            ],
            scratch_shapes=[pltpu.VMEM((160, TOKS), BF16), pltpu.VMEM((CAP, TOKS), BF16)],
        ),
        out_shape=(
            jax.ShapeDtypeStruct((32, CAP), I32),
            jax.ShapeDtypeStruct((32, 2, 128), I32),
        ),
        name="routing",
    )(valid_counts, token_ids.reshape(BLOCKS, BLOCK))


ROW_AXES = ("z", "y", "x")
FIRST = ("x", "z", "y")
SECOND = ("y", "x", "z")
STEPS = (2, 1, 3, 0)


def quarter(ref, q):
    return ref.at[pl.ds(pl.multiple_of(q * QROWS, 16), QROWS)]


ROWS = 512
SUB = 64
PLANE = TOKS + 8
STAGE = CAP + 8


def row_grads(g, v, gain):
    x = v.astype(F32)
    cen = x - jnp.mean(x, axis=1, keepdims=True)
    inv = lax.rsqrt(jnp.mean(cen * cen, axis=1, keepdims=True) + 1e-12)
    scaled = gain * g.astype(F32)
    first = jnp.mean(scaled, axis=1, keepdims=True)
    second = jnp.mean(scaled * cen, axis=1, keepdims=True) * inv
    return inv * (scaled - first - cen * (inv * second))


def table_kernel(
    tok, lab, g_hbm, v_hbm, gain_ref, out,
    gbuf, vbuf, rows, stage, box, inbox, inlab, tab, got2a, got2, u0, u1, ub0, ub1, got3, f,
    load, s1, r1, sl, rl, own1, s2a, r2a, s2, r2, s3, r3, s4, r4,
):
    x, z, y, c = place()
    barrier = pltpu.get_barrier_semaphore()
    hops = [(a, d, dc) for a in ROW_AXES for d in (1, 2, 3) for dc in (0, 1)] + [("x", 0, 1)]
    for a, d, dc in hops:
        pl.semaphore_signal(barrier, 1, device_id=shifted(a, d, dc), device_id_type=MESH)
    for e in range(4):
        pl.semaphore_signal(barrier, 1, device_id=device(z, e, y, c), device_id_type=MESH)

    def remote(src, dst, send, recv, to):
        return pltpu.make_async_remote_copy(
            src_ref=src, dst_ref=dst, send_sem=send, recv_sem=recv, device_id=to, device_id_type=MESH
        )

    def owner_of(ch, r):
        return ((z if ch == 1 else y) + r) % 4

    def loads(i, slot):
        at = pl.ds(i * ROWS, ROWS)
        return (
            pltpu.make_async_copy(g_hbm.at[at], gbuf.at[slot], load.at[0, slot]),
            pltpu.make_async_copy(v_hbm.at[at], vbuf.at[slot], load.at[1, slot]),
        )

    for copy in loads(0, 0):
        copy.start()
    for j in range(6):
        rows[pl.ds(j * PLANE + TOKS, 8), :] = jnp.zeros((8, 128), F32)
    gain = gain_ref[...].reshape(1, 768)

    def grads(i, carry):
        slot = i % 2

        @pl.when(i + 1 < TOKS // ROWS)
        def _():
            for copy in loads(i + 1, 1 - slot):
                copy.start()

        for copy in loads(i, slot):
            copy.wait()

        def sub_block(k, carry):
            at = pl.ds(pl.multiple_of(k * SUB, SUB), SUB)
            dx = row_grads(gbuf[slot, at, :], vbuf[slot, at, :], gain)
            for j in range(6):
                to = pl.multiple_of(j * PLANE + i * ROWS + k * SUB, 8)
                rows[pl.ds(to, SUB), :] = dx[:, j * 128 : (j + 1) * 128]
            return carry

        lax.fori_loop(0, ROWS // SUB, sub_block, 0, unroll=2)
        return carry

    lax.fori_loop(0, TOKS // ROWS, grads, 0)
    pl.semaphore_wait(barrier, len(hops) + 4)

    def label_copy(ch, d, dc):
        q = (coordinate(ROW_AXES[ch]) + d) % 4
        cq = (c + dc) % 2
        src = lab.at[:, q, cq] if ch == 1 else lab.at[q, :, cq]
        k = d * 2 + dc
        if k == 0:
            return pltpu.make_async_copy(src, inlab.at[ch, 0], own1.at[ch])
        return remote(src, inlab.at[ch, k], sl.at[ch, k], rl.at[ch, k], shifted(ROW_AXES[ch], d, dc))

    routes = [(d, dc) for d in (2, 1, 3, 0) for dc in (0, 1)]
    labels = {}
    for d, dc in routes:
        for ch in range(3):
            labels[ch, d, dc] = label_copy(ch, d, dc)
            labels[ch, d, dc].start()

    blocks = [(ry, rz, dc) for ry in STEPS for rz in STEPS for dc in (0, 1)]

    def row_copy(ch, b):
        ry, rz, dc = blocks[b]
        r = rz if ch == 1 else ry
        d = (rz, ry, (z + rz - x + 4) % 4)[ch]
        k = d * 2 + dc
        return remote(
            box.at[ch, b], inbox.at[ch, r, k], s1.at[ch, r, k], r1.at[ch, r, k],
            shifted(ROW_AXES[ch], d, dc),
        )

    def on_rows(b, action):
        ry, rz, dc = blocks[b]
        if rz + dc:
            action(row_copy(0, b))
        if ry + dc:
            action(row_copy(1, b))
        if dc:
            action(row_copy(2, b))
        else:

            @pl.when((z + rz) % 4 != x)
            def _():
                action(row_copy(2, b))

    for b, (ry, rz, dc) in enumerate(blocks):
        w = (z + rz) % 4 * 8 + (y + ry) % 4 * 2 + (c + dc) % 2
        at = b % 2 * 6 * STAGE

        def gather(i, carry):
            for e in range(16):
                t = tok[w, i * 16 + e]
                stage[pl.ds(at + i * 16 + e, 6, stride=STAGE), :] = rows[pl.ds(t, 6, stride=PLANE), :]
            return carry

        lax.fori_loop(0, CAP // 16, gather, 0)
        for ch in range(3):
            block = jnp.concatenate(
                [stage[pl.ds(at + (ch * 2 + h) * STAGE, CAP), :].astype(BF16) for h in range(2)], axis=1
            )
            if ch == 0 and rz + dc == 0:
                inbox[0, ry, 0] = block
            elif ch == 1 and ry + dc == 0:
                inbox[1, rz, 0] = block
            else:
                box[ch, b] = block
                if ch == 2 and dc == 0:

                    @pl.when((z + rz) % 4 == x)
                    def _():
                        inbox[2, ry, 0] = box[2, b]

        if b > 0:
            on_rows(b - 1, lambda copy: copy.start())
    on_rows(31, lambda copy: copy.start())

    def arrived(ch, r, d, dc):
        if d + dc:
            k = d * 2 + dc
            remote(
                box.at[ch, 0], inbox.at[ch, r, k], s1.at[ch, r, k], r1.at[ch, r, k],
                shifted(ROW_AXES[ch], d, dc),
            ).wait_recv()

    twos = {}
    for d, dc in routes:
        for ch in range(3):
            if d + dc:
                labels[ch, d, dc].wait_recv()
            else:
                labels[ch, d, dc].wait()
    order = [(ch, r) for r in (2, 1, 3) for ch in (0, 2)]
    order += [(1, 2), (0, 0), (1, 1), (1, 3), (2, 0), (1, 0)]
    for ch, r in order:
        if True:
            for d, dc in routes:
                arrived(ch, r, d, dc)
            w = owner_of(ch, r)

            def part(m, carry):
                ids = lax.broadcasted_iota(I32, (QROWS, 128), 0) + m * QROWS
                total = None
                for k in range(8):
                    picks = jnp.concatenate(
                        [
                            jnp.where(ids == inlab[ch, k, w, pl.ds(h, 1), :], 1.0, 0.0).astype(BF16)
                            for h in range(2)
                        ],
                        axis=1,
                    )
                    add = jnp.dot(picks, inbox[ch, r, k], preferred_element_type=F32)
                    total = add if total is None else total + add
                at = pl.ds(pl.multiple_of(m * QROWS, 16), QROWS)
                if ch > 0 and r == 0:
                    u1[ch - 1, at, :] = total
                else:
                    tab[ch, r, at, :] = total.astype(BF16)
                if ch == 0:

                    @pl.when(m == x)
                    def _():
                        u0[r] = total

                return carry

            lax.fori_loop(0, 4, part, 0)
            if ch == 0:
                for d in (2, 1, 3):
                    twos[0, r, d] = remote(
                        quarter(tab.at[0, r], (x + d) % 4), got2a.at[r, d - 1],
                        s2a.at[r, d - 1], r2a.at[r, d - 1], shifted("x", d),
                    )
                    twos[0, r, d].start()
            elif r > 0:
                twos[ch, r] = remote(
                    tab.at[ch, r], got2.at[ch - 1, r - 1],
                    s2.at[ch - 1, r - 1], r2.at[ch - 1, r - 1], shifted(FIRST[ch], r),
                )
                twos[ch, r].start()

    threes = {}
    for r in STEPS:
        for d in (2, 1, 3):
            twos[0, r, d].wait_recv()
        total = u0[r]
        for d in range(3):
            total += got2a[r, d].astype(F32)
        if r == 0:
            u0[0] = total
        else:
            ub0[r - 1] = total.astype(BF16)
            threes[0, r] = remote(
                ub0.at[r - 1], got3.at[0, r - 1], s3.at[0, r - 1], r3.at[0, r - 1], shifted("y", r)
            )
            threes[0, r].start()
    for ch in (1, 2):
        for r in (2, 1, 3):
            twos[ch, r].wait_recv()
        me = coordinate(SECOND[ch])
        for d in (2, 1, 3, 0):
            at = pl.ds(pl.multiple_of((me + d) % 4 * QROWS, 16), QROWS)
            total = u1[ch - 1, at, :]
            for e in range(3):
                total += got2[ch - 1, e, at, :].astype(F32)
            if d == 0:
                u1[ch - 1, at, :] = total
            else:
                ub1[ch - 1, d - 1] = total.astype(BF16)
                threes[ch, d] = remote(
                    ub1.at[ch - 1, d - 1], got3.at[ch, d - 1],
                    s3.at[ch, d - 1], r3.at[ch, d - 1], shifted(SECOND[ch], d),
                )
                threes[ch, d].start()

    fours = []
    for ch in range(3):
        for d in (2, 1, 3):
            threes[ch, d].wait_recv()
        if ch == 0:
            total = u0[0]
        else:
            me = coordinate(SECOND[ch])
            total = u1[ch - 1, pl.ds(pl.multiple_of(me * QROWS, 16), QROWS), :]
        for d in range(3):
            total += got3[ch, d].astype(F32)
        f[ch] = total.astype(BF16)
        if ch < 2:
            mine = out.at[pl.ds(pl.multiple_of(x * QROWS, 16), QROWS), pl.ds(ch * 256, 256)]
            mine[...] = f[ch]
            for d in (2, 1, 3):
                copy = remote(f.at[ch], mine, s4.at[ch, d], r4.at[ch, d], shifted("x", d))
                copy.start()
                fours.append(copy)

    mine = out.at[pl.ds(pl.multiple_of(z * QROWS, 16), QROWS), pl.ds(512, 256)]

    def last(e):
        return remote(f.at[2], mine, s4.at[2, e], r4.at[2, z], device((x + e) % 4, x, y, c))

    @pl.when(x == z)
    def _():
        mine[...] = f[2]

    @pl.when(x != z)
    def _():
        last(0).start()

    for e in (2, 1, 3):
        last(e).start()
    for q in range(4):

        @pl.when(jnp.logical_or(x != z, q != z))
        def _():
            remote(
                f.at[2], out.at[pl.ds(q * QROWS, QROWS), pl.ds(512, 256)],
                s4.at[2, 0], r4.at[2, q], device(x, z, y, c),
            ).wait_recv()

    for copy in fours:
        copy.wait()

    @pl.when(x != z)
    def _():
        last(0).wait_send()

    for e in (2, 1, 3):
        last(e).wait_send()
    for ch, d, dc in labels:
        if d + dc:
            labels[ch, d, dc].wait_send()
    for b in range(32):
        on_rows(b, lambda copy: copy.wait_send())
    for copy in list(twos.values()) + list(threes.values()):
        copy.wait_send()


def table_sums(tok, labels, grads, values, gain):
    any_space = pl.BlockSpec(memory_space=pl.ANY)
    dma = pltpu.SemaphoreType.DMA
    return pl.pallas_call(
        table_kernel,
        out_shape=jax.ShapeDtypeStruct((VOCAB_DEV, 768), BF16),
        in_specs=[
            pl.BlockSpec(memory_space=pltpu.SMEM),
            any_space,
            any_space,
            any_space,
            pl.BlockSpec(memory_space=pltpu.VMEM),
        ],
        out_specs=pl.BlockSpec(memory_space=pltpu.VMEM),
        scratch_shapes=[
            pltpu.VMEM((2, ROWS, 768), BF16),
            pltpu.VMEM((2, ROWS, 768), BF16),
            pltpu.VMEM((6 * PLANE, 128), F32),
            pltpu.VMEM((2 * 6 * STAGE, 128), F32),
            pltpu.VMEM((3, 32, CAP, 256), BF16),
            pltpu.VMEM((3, 4, 8, CAP, 256), BF16),
            pltpu.VMEM((3, 8, 4, 2, 128), I32),
            pltpu.VMEM((3, 4, VOCAB_DEV, 256), BF16),
            pltpu.VMEM((4, 3, QROWS, 256), BF16),
            pltpu.VMEM((2, 3, VOCAB_DEV, 256), BF16),
            pltpu.VMEM((4, QROWS, 256), F32),
            pltpu.VMEM((2, VOCAB_DEV, 256), F32),
            pltpu.VMEM((3, QROWS, 256), BF16),
            pltpu.VMEM((2, 3, QROWS, 256), BF16),
            pltpu.VMEM((3, 3, QROWS, 256), BF16),
            pltpu.VMEM((3, QROWS, 256), BF16),
            dma((2, 2)),
            dma((3, 4, 8)),
            dma((3, 4, 8)),
            dma((3, 8)),
            dma((3, 8)),
            dma((3,)),
            dma((4, 3)),
            dma((4, 3)),
            dma((2, 3)),
            dma((2, 3)),
            dma((3, 3)),
            dma((3, 3)),
            dma((3, 4)),
            dma((3, 4)),
        ],
        compiler_params=pltpu.CompilerParams(
            collective_id=0, has_side_effects=True, vmem_limit_bytes=62 << 20
        ),
        name="table_sums",
    )(tok, labels.reshape(4, 4, 2, 2, 128), grads, values, gain)


def per_device(token_ids, valid_counts, grad_output, pre_norm, norm_gain):
    tok, labels = routing(token_ids, valid_counts)
    return table_sums(tok, labels, grad_output, pre_norm, norm_gain).astype(F32)


def solution(mesh):
    in_specs = (
        P(("dp", "vocab")),
        P(("dp", "vocab")),
        P(("dp", "vocab"), None),
        P(("dp", "vocab"), None),
        P(),
    )
    return jax.shard_map(
        per_device, mesh=mesh, in_specs=in_specs, out_specs=P("vocab", None), check_vma=False
    )
```

time: 139 us -> 124 us (0.89)
  Pallas kernels: 129 us -> 120 us
  other arithmetic: 6.15 us -> 3.19 us
  local copies, waits for them, and re-layouts: 2.07 us -> 0 us
    pallas_call x1, Pallas kernels: 23.1 us -> 3.5 us  [routing(): pl.pallas_call(routing_kernel, grid_spec=pltpu.PrefetchScalarGridSpec(num...]
    pallas_call x1, Pallas kernels: 106 us -> 117 us  [table_sums(): pl.pallas_call(table_kernel, out_shape=jax.ShapeDtypeStruct((VOCAB_DEV, 7...]
    convert_element_type x7 -> x1, other arithmetic: 3.35 us -> 3.19 us  [per_device(): return table_sums(tok, labels, grad_output, pre_norm, norm_gain).astype(F32)]
where the time goes in v3:
time: 124 us; the launch traced here: 123 us
  Pallas kernels  120 us (97%)
  other arithmetic  3.19 us (3%)
    pallas_call x1, Pallas kernels, table_sums(): pl.pallas_call(table_kernel, out_shape=jax.ShapeDtypeStruct((VOCAB_DEV, 7...  117 us
    pallas_call x1, Pallas kernels, routing(): pl.pallas_call(routing_kernel, grid_spec=pltpu.PrefetchScalarGridSpec(num...  3.5 us
    convert_element_type x1, other arithmetic, per_device(): return table_sums(tok, labels, grad_output, pre_norm, norm_gain).astype(F32)  3.19 us

profile of v3, /device:TPU:2, one launch (start us, length us, event | category | flops | bytes accessed | tf_op | source)
XLA Modules:
  0.0 123.4 jit_solution(12583617069615022989)
XLA Ops:
  0.0 3.5 %routing.1 = (s32[32,256]{1,0:T(8,128)}, s32[32,2,128]{2,1,0:T(2,128)}) custom-call(s32[32]{0:T(128)} %counts.1, s32[32,128]{1,0:T(8,128)} %bitcast.3), custom_call_target="tpu_custom_call" | custom-call | tf_op jit(solution)/shard_map/routing/pallas_call | solution.py:91
  3.5 116.7 %table_sums.1 = bf16[960,768]{1,0:T(8,128)(2,1)} custom-call(s32[32,256]{1,0:T(8,128)} %get-tuple-element.7.tok, s32[4,4,2,2,128]{4,3,2,1,0:T(2,128)} %bitcast.2, bf16[4096,768]{1,0:T(8,128)(2,1)} %g_hbm.1, bf16[4096,768]{1,0:T(8,128)(2,1)} %v_hbm.1, f32[768]{0:T(1024)} %gain_ref.1), custom_call_target="tpu_custom_call" | custom-call | tf_op jit(solution)/shard_map/table_sums/pallas_call | solution.py:432
  120.2 3.2 %convert_element_type.3 = f32[960,768]{1,0:T(8,128)} convert(bf16[960,768]{1,0:T(8,128)(2,1)} %table_sums.1) | non-fusion elementwise | flops 737280 | bytes 4423680 | tf_op jit(solution)/shard_map/convert_element_type | solution.py:484

commit v4 on v3

--- a/solution.py
+++ b/solution.py
@@ -11,6 +11,8 @@
 BLOCK = 128
 CAP = 256
 QROWS = VOCAB_DEV // 4
+HALF = VOCAB_DEV // 2
+LOW, HIGH = 128, 112
 MESH = pl.DeviceIdType.MESH
 F32, BF16, I32 = jnp.float32, jnp.bfloat16, jnp.int32
 
@@ -114,12 +116,8 @@
 STEPS = (2, 1, 3, 0)
 
 
-def quarter(ref, q):
-    return ref.at[pl.ds(pl.multiple_of(q * QROWS, 16), QROWS)]
-
-
 ROWS = 512
-SUB = 64
+SUB = 128
 PLANE = TOKS + 8
 STAGE = CAP + 8
 
@@ -136,7 +134,7 @@
 
 def table_kernel(
     tok, lab, g_hbm, v_hbm, gain_ref, out,
-    gbuf, vbuf, rows, stage, box, inbox, inlab, tab, got2a, got2, u0, u1, ub0, ub1, got3, f,
+    rows, stage, box, inbox, inlab, tab, got2a, got2, via0, via1, via2, mid0, mid1, mid2, u0, u1, ub0, ub1, got3, f,
     load, s1, r1, sl, rl, own1, s2a, r2a, s2, r2, s3, r3, s4, r4,
 ):
     x, z, y, c = place()
@@ -155,33 +153,37 @@
     def owner_of(ch, r):
         return ((z if ch == 1 else y) + r) % 4
 
-    def loads(i, slot):
-        at = pl.ds(i * ROWS, ROWS)
-        return (
-            pltpu.make_async_copy(g_hbm.at[at], gbuf.at[slot], load.at[0, slot]),
-            pltpu.make_async_copy(v_hbm.at[at], vbuf.at[slot], load.at[1, slot]),
-        )
-
-    for copy in loads(0, 0):
-        copy.start()
+    def loads(i):
+        at = pl.ds(i * 2, 2)
+        return [
+            pltpu.make_async_copy(
+                src.at[at, :, pl.ds(ch * 256, 256)],
+                box.at[ch, pl.ds(half * 16 + i * 2, 2)],
+                load.at[i, half, ch],
+            )
+            for half, src in enumerate((g_hbm, v_hbm))
+            for ch in range(3)
+        ]
+
+    for i in range(TOKS // ROWS):
+        for copy in loads(i):
+            copy.start()
     for j in range(6):
         rows[pl.ds(j * PLANE + TOKS, 8), :] = jnp.zeros((8, 128), F32)
     gain = gain_ref[...].reshape(1, 768)
 
     def grads(i, carry):
-        slot = i % 2
-
-        @pl.when(i + 1 < TOKS // ROWS)
-        def _():
-            for copy in loads(i + 1, 1 - slot):
-                copy.start()
-
-        for copy in loads(i, slot):
+        for copy in loads(i):
             copy.wait()
 
         def sub_block(k, carry):
-            at = pl.ds(pl.multiple_of(k * SUB, SUB), SUB)
-            dx = row_grads(gbuf[slot, at, :], vbuf[slot, at, :], gain)
+            at = pl.ds(pl.multiple_of(k % (CAP // SUB) * SUB, SUB), SUB)
+            block = i * 2 + k // (CAP // SUB)
+            g, v = (
+                jnp.concatenate([box[ch, half + block, at, :] for ch in range(3)], axis=1)
+                for half in (0, 16)
+            )
+            dx = row_grads(g, v, gain)
             for j in range(6):
                 to = pl.multiple_of(j * PLANE + i * ROWS + k * SUB, 8)
                 rows[pl.ds(to, SUB), :] = dx[:, j * 128 : (j + 1) * 128]
@@ -274,69 +276,151 @@
                 shifted(ROW_AXES[ch], d, dc),
             ).wait_recv()
 
-    twos = {}
+    twos = []
+
+    def send2(ch, r, kind, src, dst):
+        send, recv = (s2a.at[r, kind], r2a.at[r, kind]) if ch == 0 else (s2.at[ch - 1, kind], r2.at[ch - 1, kind])
+        copy = remote(src, dst, send, recv, shifted(FIRST[ch], 3 if kind % 2 else 1))
+        copy.start()
+        twos.append(copy)
+        return copy
+
+    def rows_of(q, first, count):
+        return pl.ds(pl.multiple_of(q * QROWS + first, 16), count)
+
+    north, south = (x + 1) % 4, (x + 3) % 4
+    relays = {}
+    direct = {}
+
+    def start_sums(ch, r):
+        if ch == 0:
+            t = tab.at[0, r]
+            relays[0, r] = (
+                send2(0, r, 0, t.at[rows_of((x + 2) % 4, 0, LOW)], via0.at[r]),
+                send2(0, r, 1, t.at[rows_of((x + 2) % 4, LOW, HIGH)], via1.at[r]),
+            )
+            direct[0, r] = [
+                send2(0, r, 2, t.at[rows_of(north, LOW, HIGH)], got2a.at[r, 0, pl.ds(LOW, HIGH)]),
+                send2(0, r, 3, t.at[rows_of(south, 0, LOW)], got2a.at[r, 1, pl.ds(0, LOW)]),
+            ]
+        elif r == 2:
+            relays[ch] = (
+                send2(ch, r, 0, tab.at[ch, 2, pl.ds(0, HALF)], via2.at[ch - 1, 0]),
+                send2(ch, r, 1, tab.at[ch, 2, pl.ds(HALF, HALF)], via2.at[ch - 1, 1]),
+            )
+            direct[ch] = []
+        elif r == 1:
+            direct[ch].append(
+                send2(ch, r, 2, tab.at[ch, 1, pl.ds(HALF, HALF)], got2.at[ch - 1, 0, pl.ds(HALF, HALF)])
+            )
+        elif r == 3:
+            direct[ch].append(
+                send2(ch, r, 3, tab.at[ch, 3, pl.ds(0, HALF)], got2.at[ch - 1, 1, pl.ds(0, HALF)])
+            )
+
+    def relay(ch, r=None):
+        if ch == 0:
+            t = tab.at[0, r]
+            relays[0, r][0].wait_recv()
+            at = rows_of(north, 0, LOW)
+            t[at, :] = (mid0[r] + via0[r].astype(F32)).astype(BF16)
+            direct[0, r].append(send2(0, r, 4, t.at[at], got2a.at[r, 0, pl.ds(0, LOW)]))
+            relays[0, r][1].wait_recv()
+            at = rows_of(south, LOW, HIGH)
+            t[at, :] = (mid1[r] + via1[r].astype(F32)).astype(BF16)
+            direct[0, r].append(send2(0, r, 5, t.at[at], got2a.at[r, 1, pl.ds(LOW, HIGH)]))
+        else:
+            for side, (w, first) in enumerate(((1, 0), (3, HALF))):
+                relays[ch][side].wait_recv()
+                at = pl.ds(first, HALF)
+                tab[ch, w, at, :] = (
+                    mid2[ch - 1, side] + via2[ch - 1, side].astype(F32)
+                ).astype(BF16)
+                direct[ch].append(
+                    send2(ch, w, 4 + side, tab.at[ch, w, at], got2.at[ch - 1, side, at])
+                )
+
     for d, dc in routes:
         for ch in range(3):
             if d + dc:
                 labels[ch, d, dc].wait_recv()
             else:
                 labels[ch, d, dc].wait()
-    order = [(ch, r) for r in (2, 1, 3) for ch in (0, 2)]
-    order += [(1, 2), (0, 0), (1, 1), (1, 3), (2, 0), (1, 0)]
-    for ch, r in order:
-        if True:
-            for d, dc in routes:
-                arrived(ch, r, d, dc)
-            w = owner_of(ch, r)
-
-            def part(m, carry):
-                ids = lax.broadcasted_iota(I32, (QROWS, 128), 0) + m * QROWS
-                total = None
-                for k in range(8):
-                    picks = jnp.concatenate(
-                        [
-                            jnp.where(ids == inlab[ch, k, w, pl.ds(h, 1), :], 1.0, 0.0).astype(BF16)
-                            for h in range(2)
-                        ],
-                        axis=1,
-                    )
-                    add = jnp.dot(picks, inbox[ch, r, k], preferred_element_type=F32)
-                    total = add if total is None else total + add
-                at = pl.ds(pl.multiple_of(m * QROWS, 16), QROWS)
-                if ch > 0 and r == 0:
-                    u1[ch - 1, at, :] = total
-                else:
+
+    def partial_table(ch, r):
+        for d, dc in routes:
+            arrived(ch, r, d, dc)
+        w = owner_of(ch, r)
+
+        def part(m, carry):
+            ids = lax.broadcasted_iota(I32, (QROWS, 128), 0) + m * QROWS
+            total = None
+            for k in range(8):
+                picks = jnp.concatenate(
+                    [
+                        jnp.where(ids == inlab[ch, k, w, pl.ds(h, 1), :], 1.0, 0.0).astype(BF16)
+                        for h in range(2)
+                    ],
+                    axis=1,
+                )
+                add = jnp.dot(picks, inbox[ch, r, k], preferred_element_type=F32)
+                total = add if total is None else total + add
+            at = pl.ds(pl.multiple_of(m * QROWS, 16), QROWS)
+            if ch > 0 and r == 0:
+                u1[ch - 1, at, :] = total
+            elif ch > 0 and r != 2:
+                side, summed = (0, m < 2) if r == 1 else (1, m >= 2)
+
+                @pl.when(summed)
+                def _():
+                    mid2[ch - 1, side, pl.ds(pl.multiple_of(m % 2 * QROWS, 16), QROWS), :] = total
+
+                @pl.when(jnp.logical_not(summed))
+                def _():
                     tab[ch, r, at, :] = total.astype(BF16)
-                if ch == 0:
-
-                    @pl.when(m == x)
-                    def _():
-                        u0[r] = total
-
-                return carry
-
-            lax.fori_loop(0, 4, part, 0)
+
+            else:
+                tab[ch, r, at, :] = total.astype(BF16)
             if ch == 0:
-                for d in (2, 1, 3):
-                    twos[0, r, d] = remote(
-                        quarter(tab.at[0, r], (x + d) % 4), got2a.at[r, d - 1],
-                        s2a.at[r, d - 1], r2a.at[r, d - 1], shifted("x", d),
-                    )
-                    twos[0, r, d].start()
-            elif r > 0:
-                twos[ch, r] = remote(
-                    tab.at[ch, r], got2.at[ch - 1, r - 1],
-                    s2.at[ch - 1, r - 1], r2.at[ch - 1, r - 1], shifted(FIRST[ch], r),
-                )
-                twos[ch, r].start()
+
+                @pl.when(m == x)
+                def _():
+                    u0[r] = total
+
+                @pl.when(m == north)
+                def _():
+                    mid0[r] = total[:LOW]
+
+                @pl.when(m == south)
+                def _():
+                    mid1[r] = total[LOW:]
+
+            return carry
+
+        lax.fori_loop(0, 4, part, 0)
+        start_sums(ch, r)
+
+    for r in (2, 1, 3):
+        partial_table(0, r)
+        partial_table(2, r)
+    partial_table(1, 2)
+    partial_table(0, 0)
+    partial_table(1, 1)
+    partial_table(1, 3)
+    relay(0, 2)
+    relay(0, 1)
+    relay(2)
+    partial_table(2, 0)
+    partial_table(1, 0)
+    relay(0, 3)
+    relay(1)
+    relay(0, 0)
 
     threes = {}
     for r in STEPS:
-        for d in (2, 1, 3):
-            twos[0, r, d].wait_recv()
-        total = u0[r]
-        for d in range(3):
-            total += got2a[r, d].astype(F32)
+        for copy in direct[0, r]:
+            copy.wait_recv()
+        total = u0[r] + got2a[r, 0].astype(F32) + got2a[r, 1].astype(F32)
         if r == 0:
             u0[0] = total
         else:
@@ -345,14 +429,14 @@
                 ub0.at[r - 1], got3.at[0, r - 1], s3.at[0, r - 1], r3.at[0, r - 1], shifted("y", r)
             )
             threes[0, r].start()
-    for ch in (1, 2):
-        for r in (2, 1, 3):
-            twos[ch, r].wait_recv()
+    for ch in (2, 1):
+        for copy in direct[ch]:
+            copy.wait_recv()
         me = coordinate(SECOND[ch])
         for d in (2, 1, 3, 0):
             at = pl.ds(pl.multiple_of((me + d) % 4 * QROWS, 16), QROWS)
             total = u1[ch - 1, at, :]
-            for e in range(3):
+            for e in range(2):
                 total += got2[ch - 1, e, at, :].astype(F32)
             if d == 0:
                 u1[ch - 1, at, :] = total
@@ -364,8 +448,26 @@
                 )
                 threes[ch, d].start()
 
+    third = out.at[rows_of(z, 0, QROWS), pl.ds(512, 256)]
+
+    def last(e):
+        return remote(f.at[2], third, s4.at[2, e], r4.at[2, z], device((x + e) % 4, x, y, c))
+
+    def last_chunk_starts():
+        @pl.when(x == z)
+        def _():
+            third[...] = f[2]
+
+        @pl.when(x != z)
+        def _():
+            last(0).start()
+
+        for e in (2, 1, 3):
+            last(e).start()
+
     fours = []
-    for ch in range(3):
+    fulls = {}
+    for ch in (0, 2, 1):
         for d in (2, 1, 3):
             threes[ch, d].wait_recv()
         if ch == 0:
@@ -377,28 +479,24 @@
             total += got3[ch, d].astype(F32)
         f[ch] = total.astype(BF16)
         if ch < 2:
-            mine = out.at[pl.ds(pl.multiple_of(x * QROWS, 16), QROWS), pl.ds(ch * 256, 256)]
+            mine = out.at[rows_of(x, 0, QROWS), pl.ds(ch * 256, 256)]
             mine[...] = f[ch]
-            for d in (2, 1, 3):
-                copy = remote(f.at[ch], mine, s4.at[ch, d], r4.at[ch, d], shifted("x", d))
+            fulls[ch] = [
+                remote(f.at[ch], mine, s4.at[ch, e], r4.at[ch, e], shifted("x", d))
+                for e, d in enumerate((1, 3))
+            ]
+            for copy in fulls[ch]:
                 copy.start()
-                fours.append(copy)
-
-    mine = out.at[pl.ds(pl.multiple_of(z * QROWS, 16), QROWS), pl.ds(512, 256)]
-
-    def last(e):
-        return remote(f.at[2], mine, s4.at[2, e], r4.at[2, z], device((x + e) % 4, x, y, c))
-
-    @pl.when(x == z)
-    def _():
-        mine[...] = f[2]
-
-    @pl.when(x != z)
-    def _():
-        last(0).start()
-
-    for e in (2, 1, 3):
-        last(e).start()
+        else:
+            last_chunk_starts()
+    for ch in (0, 1):
+        for e, (q, first, count, d) in enumerate(((south, 0, LOW, 1), (north, LOW, HIGH, 3))):
+            fulls[ch][e].wait_recv()
+            piece = out.at[rows_of(q, first, count), pl.ds(ch * 256, 256)]
+            copy = remote(piece, piece, s4.at[ch, 2 + e], r4.at[ch, 2 + e], shifted("x", d))
+            copy.start()
+            fours.append(copy)
+
     for q in range(4):
 
         @pl.when(jnp.logical_or(x != z, q != z))
@@ -422,7 +520,7 @@
             labels[ch, d, dc].wait_send()
     for b in range(32):
         on_rows(b, lambda copy: copy.wait_send())
-    for copy in list(twos.values()) + list(threes.values()):
+    for copy in twos + list(threes.values()) + fulls[0] + fulls[1]:
         copy.wait_send()
 
 
@@ -441,32 +539,36 @@
         ],
         out_specs=pl.BlockSpec(memory_space=pltpu.VMEM),
         scratch_shapes=[
-            pltpu.VMEM((2, ROWS, 768), BF16),
-            pltpu.VMEM((2, ROWS, 768), BF16),
             pltpu.VMEM((6 * PLANE, 128), F32),
             pltpu.VMEM((2 * 6 * STAGE, 128), F32),
             pltpu.VMEM((3, 32, CAP, 256), BF16),
             pltpu.VMEM((3, 4, 8, CAP, 256), BF16),
             pltpu.VMEM((3, 8, 4, 2, 128), I32),
             pltpu.VMEM((3, 4, VOCAB_DEV, 256), BF16),
-            pltpu.VMEM((4, 3, QROWS, 256), BF16),
-            pltpu.VMEM((2, 3, VOCAB_DEV, 256), BF16),
+            pltpu.VMEM((4, 2, QROWS, 256), BF16),
+            pltpu.VMEM((2, 2, VOCAB_DEV, 256), BF16),
+            pltpu.VMEM((4, LOW, 256), BF16),
+            pltpu.VMEM((4, HIGH, 256), BF16),
+            pltpu.VMEM((2, 2, HALF, 256), BF16),
+            pltpu.VMEM((4, LOW, 256), F32),
+            pltpu.VMEM((4, HIGH, 256), F32),
+            pltpu.VMEM((2, 2, HALF, 256), F32),
             pltpu.VMEM((4, QROWS, 256), F32),
             pltpu.VMEM((2, VOCAB_DEV, 256), F32),
             pltpu.VMEM((3, QROWS, 256), BF16),
             pltpu.VMEM((2, 3, QROWS, 256), BF16),
             pltpu.VMEM((3, 3, QROWS, 256), BF16),
             pltpu.VMEM((3, QROWS, 256), BF16),
-            dma((2, 2)),
+            dma((TOKS // ROWS, 2, 3)),
             dma((3, 4, 8)),
             dma((3, 4, 8)),
             dma((3, 8)),
             dma((3, 8)),
             dma((3,)),
-            dma((4, 3)),
-            dma((4, 3)),
-            dma((2, 3)),
-            dma((2, 3)),
+            dma((4, 6)),
+            dma((4, 6)),
+            dma((2, 6)),
+            dma((2, 6)),
             dma((3, 3)),
             dma((3, 3)),
             dma((3, 4)),
@@ -476,7 +578,9 @@
             collective_id=0, has_side_effects=True, vmem_limit_bytes=62 << 20
         ),
         name="table_sums",
-    )(tok, labels.reshape(4, 4, 2, 2, 128), grads, values, gain)
+    )(
+        tok, labels.reshape(4, 4, 2, 2, 128), grads.reshape(16, CAP, 768), values.reshape(16, CAP, 768), gain
+    )
 
 
 def per_device(token_ids, valid_counts, grad_output, pre_norm, norm_gain):

time: 124 us -> 117 us (0.944)
  the two profiles are of different devices: /device:TPU:2 before, /device:TPU:72 now
where the time goes in v4:
time: 117 us
  Pallas kernels  114 us (97%)
  other arithmetic  3.19 us (3%)
    pallas_call x1, Pallas kernels, table_sums(): pl.pallas_call(table_kernel, out_shape=jax.ShapeDtypeStruct((VOCAB_DEV, 7...  110 us
    pallas_call x1, Pallas kernels, routing(): pl.pallas_call(routing_kernel, grid_spec=pltpu.PrefetchScalarGridSpec(num...  3.5 us
    convert_element_type x1, other arithmetic, per_device(): return table_sums(tok, labels, grad_output, pre_norm, norm_gain).astype(F32)  3.19 us

profile of v4, /device:TPU:72, one launch (start us, length us, event | category | flops | bytes accessed | tf_op | source)
XLA Modules:
  0.0 116.8 jit_solution(6735011238212480810)
XLA Ops:
  0.0 3.5 %routing.1 = (s32[32,256]{1,0:T(8,128)}, s32[32,2,128]{2,1,0:T(2,128)}) custom-call(s32[32]{0:T(128)} %counts.1, s32[32,128]{1,0:T(8,128)} %bitcast.7), custom_call_target="tpu_custom_call" | custom-call | tf_op jit(solution)/shard_map/routing/pallas_call | solution.py:93
  3.5 110.1 %table_sums.1 = bf16[960,768]{1,0:T(8,128)(2,1)} custom-call(s32[32,256]{1,0:T(8,128)} %get-tuple-element.7.tok, s32[4,4,2,2,128]{4,3,2,1,0:T(2,128)} %bitcast.6, bf16[16,256,768]{2,1,0:T(8,128)(2,1)} %bitcast.4, bf16[16,256,768]{2,1,0:T(8,128)(2,1)} %bitcast.5, f32[768]{0:T(1024)} %gain_ref.1), custom_call_target="tpu_custom_call" | custom-call | tf_op jit(solution)/shard_map/table_sums/pallas_call | solution.py:530
  113.6 3.2 %convert_element_type.3 = f32[960,768]{1,0:T(8,128)} convert(bf16[960,768]{1,0:T(8,128)(2,1)} %table_sums.1) | non-fusion elementwise | flops 737280 | bytes 4423680 | tf_op jit(solution)/shard_map/convert_element_type | solution.py:588

commit v5 on v4

--- a/solution.py
+++ b/solution.py
@@ -83,10 +83,11 @@
         weights[...], slots[...], (((1,), (1,)), ((), ())), preferred_element_type=F32
     )
     used, high, low, block, place_in = (table[p * 32 : (p + 1) * 32] for p in range(5))
+    toks = jnp.where(used > 0.5, block * 64.0 + place_in, float(TOKS)).astype(I32)
     labels = jnp.where(used > 0.5, high * 32.0 + low, -1.0).astype(I32)
     for h in range(2):
         lab_ref[:, h, :] = labels[:, h * 128 : (h + 1) * 128]
-    tok_ref[...] = jnp.where(used > 0.5, block * 64.0 + place_in, float(TOKS)).astype(I32)
+        tok_ref[:, h, :] = toks[:, h * 128 : (h + 1) * 128]
 
 
 def routing(token_ids, valid_counts):
@@ -96,16 +97,10 @@
             num_scalar_prefetch=1,
             grid=(1,),
             in_specs=[pl.BlockSpec((BLOCKS, BLOCK), lambda i, _: (0, 0))],
-            out_specs=[
-                pl.BlockSpec((32, CAP), lambda i, _: (0, 0)),
-                pl.BlockSpec((32, 2, 128), lambda i, _: (0, 0, 0)),
-            ],
+            out_specs=[pl.BlockSpec((32, 2, 128), lambda i, _: (0, 0, 0))] * 2,
             scratch_shapes=[pltpu.VMEM((160, TOKS), BF16), pltpu.VMEM((CAP, TOKS), BF16)],
         ),
-        out_shape=(
-            jax.ShapeDtypeStruct((32, CAP), I32),
-            jax.ShapeDtypeStruct((32, 2, 128), I32),
-        ),
+        out_shape=(jax.ShapeDtypeStruct((32, 2, 128), I32),) * 2,
         name="routing",
     )(valid_counts, token_ids.reshape(BLOCKS, BLOCK))
 
@@ -133,9 +128,9 @@
 
 
 def table_kernel(
-    tok, lab, g_hbm, v_hbm, gain_ref, out,
-    rows, stage, box, inbox, inlab, tab, got2a, got2, via0, via1, via2, mid0, mid1, mid2, u0, u1, ub0, ub1, got3, f,
-    load, s1, r1, sl, rl, own1, s2a, r2a, s2, r2, s3, r3, s4, r4,
+    tok_hbm, lab, g_hbm, v_hbm, gain_ref, out,
+    tok, rows, stage, box, inbox, inlab, tab, got2a, got2, via0, via1, via2, mid0, mid1, mid2, u0, u1, ub0, ub1, got3, f,
+    load, tok_sem, s1, r1, sl, rl, own1, s2a, r2a, s2, r2, s3, r3, s4, r4,
 ):
     x, z, y, c = place()
     barrier = pltpu.get_barrier_semaphore()
@@ -165,9 +160,12 @@
             for ch in range(3)
         ]
 
+    tok_copy = pltpu.make_async_copy(tok_hbm, tok, tok_sem.at[0])
     for i in range(TOKS // ROWS):
         for copy in loads(i):
             copy.start()
+        if i == 0:
+            tok_copy.start()
     for j in range(6):
         rows[pl.ds(j * PLANE + TOKS, 8), :] = jnp.zeros((8, 128), F32)
     gain = gain_ref[...].reshape(1, 768)
@@ -193,6 +191,7 @@
         return carry
 
     lax.fori_loop(0, TOKS // ROWS, grads, 0)
+    tok_copy.wait()
     pl.semaphore_wait(barrier, len(hops) + 4)
 
     def label_copy(ch, d, dc):
@@ -243,7 +242,7 @@
 
         def gather(i, carry):
             for e in range(16):
-                t = tok[w, i * 16 + e]
+                t = tok[w * CAP + i * 16 + e]
                 stage[pl.ds(at + i * 16 + e, 6, stride=STAGE), :] = rows[pl.ds(t, 6, stride=PLANE), :]
             return carry
 
@@ -531,7 +530,7 @@
         table_kernel,
         out_shape=jax.ShapeDtypeStruct((VOCAB_DEV, 768), BF16),
         in_specs=[
-            pl.BlockSpec(memory_space=pltpu.SMEM),
+            any_space,
             any_space,
             any_space,
             any_space,
@@ -539,6 +538,7 @@
         ],
         out_specs=pl.BlockSpec(memory_space=pltpu.VMEM),
         scratch_shapes=[
+            pltpu.SMEM((32 * CAP,), I32),
             pltpu.VMEM((6 * PLANE, 128), F32),
             pltpu.VMEM((2 * 6 * STAGE, 128), F32),
             pltpu.VMEM((3, 32, CAP, 256), BF16),
@@ -560,6 +560,7 @@
             pltpu.VMEM((3, 3, QROWS, 256), BF16),
             pltpu.VMEM((3, QROWS, 256), BF16),
             dma((TOKS // ROWS, 2, 3)),
+            dma((1,)),
             dma((3, 4, 8)),
             dma((3, 4, 8)),
             dma((3, 8)),
@@ -579,7 +580,7 @@
         ),
         name="table_sums",
     )(
-        tok, labels.reshape(4, 4, 2, 2, 128), grads.reshape(16, CAP, 768), values.reshape(16, CAP, 768), gain
+        tok.reshape(32 * CAP), labels.reshape(4, 4, 2, 2, 128), grads.reshape(16, CAP, 768), values.reshape(16, CAP, 768), gain
     )
 
 

time: 117 us -> 113 us (0.966)
  the two profiles are of different devices: /device:TPU:72 before, /device:TPU:2 now
where the time goes in v5:
time: 113 us; the launch traced here: 112 us
  Pallas kernels  109 us (96%)
  other arithmetic  3.19 us (3%)
    pallas_call x1, Pallas kernels, table_sums(): pl.pallas_call(table_kernel, out_shape=jax.ShapeDtypeStruct((VOCAB_DEV, 7...  105 us
    pallas_call x1, Pallas kernels, routing(): pl.pallas_call(routing_kernel, grid_spec=pltpu.PrefetchScalarGridSpec(num...  3.51 us
    convert_element_type x1, other arithmetic, per_device(): return table_sums(tok, labels, grad_output, pre_norm, norm_gain).astype(F32)  3.19 us

profile of v5, /device:TPU:2, one launch (start us, length us, event | category | flops | bytes accessed | tf_op | source)
XLA Modules:
  0.0 112.0 jit_solution(11695267699977541111)
XLA Ops:
  0.0 3.5 %routing.1 = (s32[32,2,128]{2,1,0:T(2,128)}, s32[32,2,128]{2,1,0:T(2,128)}) custom-call(s32[32]{0:T(128)} %counts.1, s32[32,128]{1,0:T(8,128)} %bitcast.9), custom_call_target="tpu_custom_call" | custom-call | tf_op jit(solution)/shard_map/routing/pallas_call | solution.py:94
  3.5 105.2 %table_sums.1 = bf16[960,768]{1,0:T(8,128)(2,1)} custom-call(s32[8192]{0:T(1024)} %bitcast.7, s32[4,4,2,2,128]{4,3,2,1,0:T(2,128)} %bitcast.8, bf16[16,256,768]{2,1,0:T(8,128)(2,1)} %bitcast.5, bf16[16,256,768]{2,1,0:T(8,128)(2,1)} %bitcast.6, f32[768]{0:T(1024)} %gain_ref.1), custom_call_target="tpu_custom_call" | custom-call | tf_op jit(solution)/shard_map/table_sums/pallas_call | solution.py:529
  108.8 3.2 %convert_element_type.3 = f32[960,768]{1,0:T(8,128)} convert(bf16[960,768]{1,0:T(8,128)(2,1)} %table_sums.1) | non-fusion elementwise | flops 737280 | bytes 4423680 | tf_op jit(solution)/shard_map/convert_element_type | solution.py:589

commit v6 on v5

--- a/solution.py
+++ b/solution.py
@@ -93,13 +93,9 @@
 def routing(token_ids, valid_counts):
     return pl.pallas_call(
         routing_kernel,
-        grid_spec=pltpu.PrefetchScalarGridSpec(
-            num_scalar_prefetch=1,
-            grid=(1,),
-            in_specs=[pl.BlockSpec((BLOCKS, BLOCK), lambda i, _: (0, 0))],
-            out_specs=[pl.BlockSpec((32, 2, 128), lambda i, _: (0, 0, 0))] * 2,
-            scratch_shapes=[pltpu.VMEM((160, TOKS), BF16), pltpu.VMEM((CAP, TOKS), BF16)],
-        ),
+        in_specs=[pl.BlockSpec(memory_space=pltpu.SMEM), pl.BlockSpec(memory_space=pltpu.VMEM)],
+        out_specs=[pl.BlockSpec(memory_space=pltpu.VMEM)] * 2,
+        scratch_shapes=[pltpu.VMEM((160, TOKS), BF16), pltpu.VMEM((CAP, TOKS), BF16)],
         out_shape=(jax.ShapeDtypeStruct((32, 2, 128), I32),) * 2,
         name="routing",
     )(valid_counts, token_ids.reshape(BLOCKS, BLOCK))
@@ -466,7 +462,7 @@
 
     fours = []
     fulls = {}
-    for ch in (0, 2, 1):
+    for ch in (0, 1, 2):
         for d in (2, 1, 3):
             threes[ch, d].wait_recv()
         if ch == 0:

time: 113 us -> 111 us (0.982)
  Pallas kernels: 109 us -> 107 us
    pallas_call x1, Pallas kernels: 105 us -> 104 us  [table_sums(): pl.pallas_call(table_kernel, out_shape=jax.ShapeDtypeStruct((VOCAB_DEV, 7...]
where the time goes in v6:
time: 111 us; the launch traced here: 110 us
  Pallas kernels  107 us (96%)
  other arithmetic  3.19 us (3%)
    pallas_call x1, Pallas kernels, table_sums(): pl.pallas_call(table_kernel, out_shape=jax.ShapeDtypeStruct((VOCAB_DEV, 7...  104 us
    convert_element_type x1, other arithmetic, per_device(): return table_sums(tok, labels, grad_output, pre_norm, norm_gain).astype(F32)  3.19 us
    pallas_call x1, Pallas kernels, routing(): pl.pallas_call(routing_kernel, in_specs=[pl.BlockSpec(memory_space=pltpu....  2.84 us

profile of v6, /device:TPU:2, one launch (start us, length us, event | category | flops | bytes accessed | tf_op | source)
XLA Modules:
  0.0 110.1 jit_solution(12563896530095223731)
XLA Ops:
  0.0 2.8 %routing.1 = (s32[32,2,128]{2,1,0:T(2,128)}, s32[32,2,128]{2,1,0:T(2,128)}) custom-call(s32[32]{0:T(128)} %counts.1, s32[32,128]{1,0:T(8,128)} %bitcast.9), custom_call_target="tpu_custom_call" | custom-call | tf_op jit(solution)/shard_map/routing/pallas_call | solution.py:94
  2.8 104.1 %table_sums.1 = bf16[960,768]{1,0:T(8,128)(2,1)} custom-call(s32[8192]{0:T(1024)} %bitcast.7, s32[4,4,2,2,128]{4,3,2,1,0:T(2,128)} %bitcast.8, bf16[16,256,768]{2,1,0:T(8,128)(2,1)} %bitcast.5, bf16[16,256,768]{2,1,0:T(8,128)(2,1)} %bitcast.6, f32[768]{0:T(1024)} %gain_ref.1), custom_call_target="tpu_custom_call" | custom-call | tf_op jit(solution)/shard_map/table_sums/pallas_call | solution.py:525
  106.9 3.2 %convert_element_type.3 = f32[960,768]{1,0:T(8,128)} convert(bf16[960,768]{1,0:T(8,128)(2,1)} %table_sums.1) | non-fusion elementwise | flops 737280 | bytes 4423680 | tf_op jit(solution)/shard_map/convert_element_type | solution.py:585
